TPU v7x, 32 devices: a whole 2x2x4 slice. The times are simulated.
32 devices in a mesh: gx: 4 (over y, x), gy: 4 (over z), ma: 2 (over core).
Axes of the slice: x: 2, y: 2, z: 4, core: 2. Of those that a mesh axis runs over, the one named last changes fastest.
Arguments:
- alpha_fields: bfloat16 [80, 2, 512, 512], P('ma', None, 'gy', 'gx'), may hold values from -6 to 6
- member_perts: bfloat16 [80, 2, 512, 512], P('ma', None, 'gy', 'gx'), may hold values from -0.625 to 0.625
- band_widths: int32 [2], replicated, may hold values from 2 to 8
- lat_index: int32 [1024], P('gy'), may hold values from 0 to 510, as said below
- lat_weight: float32 [1024], P('gy'), may hold values from 0 to 1
- lon_index: int32 [1024], P('gx'), may hold values from 0 to 511, as said below
- lon_weight: float32 [1024], P('gx'), may hold values from 0 to 1
- innovation: float32 [2, 1024, 1024], P(None, 'gy', 'gx'), may hold values from -6 to 6
- obs_weight: float32 [2, 1024, 1024], P(None, 'gy', 'gx'), may hold values from 0.1 to 1
Outputs:
- increment: float32 [2, 1024, 1024], P(None, 'gy', 'gx')
- gradient: float32 [80, 2, 512, 512], P('ma', None, 'gy', 'gx')
Inputs may be any that keep to these rules, and one draw needn't show every extreme that they name: lat_index[p] is p // 2 - 1 or p // 2, clamped to 0 .. 510. lon_index[q] is q // 2 - 1 or q // 2, taken modulo 512.
All inputs are finite; a program needn't handle non-finite values.
Results may differ from a plain program's by a relative error of at most 0.0003.
Values may be sent and summed in bfloat16 or wider, within the bound.
A program may use at most 128 MiB of HBM per device.

v0:
```python
import jax
import jax.numpy as jnp
from jax import lax
from jax.experimental import pallas as pl
from jax.experimental.pallas import tpu as pltpu
from jax.sharding import PartitionSpec as P

HB = 8
GROUP = 8
FR = 24
FC = 32
CR = 16
STRIP = 24
REACH = HB + 10
MESH = pl.DeviceIdType.MESH
VMEM_LIMIT = 60 * 2**20
F32 = jnp.float32
BF16 = jnp.bfloat16


def iota(shape, dim):
    return lax.broadcasted_iota(jnp.int32, shape, dim)


def dot(a, b):
    return jnp.dot(a, b, preferred_element_type=F32)


def split(value):
    high = value.astype(BF16)
    return high, (value - high.astype(F32)).astype(BF16)


def dot3(a, b):
    return dot(a[0], b[0]) + dot(a[1], b[0]) + dot(a[0], b[1])


def rows_of(*parts):
    return jnp.concatenate(parts, axis=0)


def lanes_of(*parts):
    return jnp.concatenate(parts, axis=1)


def natural(x, rows):
    return rows_of(x[rows : rows + HB], x[:rows], x[rows + HB :])


def place(order, size, width):
    return jnp.where(order < size, order, jnp.where(order < size + width, order - size - width, order - width))


def tap_value(distance, spread, scale):
    d = distance.astype(F32)
    value = jnp.exp(-(d * d) / (2.0 * spread * spread)) * scale
    return jnp.where(jnp.abs(distance) <= HB, value, 0.0)


def tap_scale(spread):
    lane = iota((8, 128), 1)
    d = (lane - HB).astype(F32)
    shape = jnp.where(lane <= 2 * HB, jnp.exp(-(d * d) / (2.0 * spread * spread)), 0.0)
    return (1.0 / jnp.sqrt(jnp.sum(shape * shape, axis=1, keepdims=True)))[:1]


def lat_taps(spread, scale, height, deep, offset, width):
    i, c = iota((height, width), 0), iota((height, width), 1)
    r = jnp.where(c >= 2 * deep, c - 2 * deep, jnp.where(c >= deep, c - deep, c))
    value = tap_value(r - i + offset, spread, scale)
    high = value.astype(BF16).astype(F32)
    return jnp.where((c >= deep) & (c < 2 * deep), value - high, high).astype(BF16)


def side_cell(lane, level, cols):
    west = lane // (GROUP * HB) == level
    return jnp.where(west, lane % HB - HB, cols + lane % HB)


def weigh(cell, index, weight):
    cell = cell.astype(F32)
    return jnp.where(cell == index, 1.0 - weight, 0.0) + jnp.where(cell == index + 1.0, weight, 0.0)


class Link:
    def __init__(self, axis, step, src, dst, send, recv, slot, also=None):
        me, count = lax.axis_index(axis), lax.axis_size(axis)
        target = me + step
        self.sends = self.gets = None
        if axis == "gx":
            target = lax.rem(target + count, count)
        elif axis == "gy":
            self.sends = (target >= 0) & (target < count)
            self.gets = (me - step >= 0) & (me - step < count)
        self.dst = dst
        device = {axis: target} if also is None else {axis: target, "ma": also}
        self.copy = pltpu.make_async_remote_copy(
            src_ref=src,
            dst_ref=dst,
            send_sem=send.at[slot],
            recv_sem=recv.at[slot],
            device_id=device,
            device_id_type=MESH,
        )

    def start(self):
        if self.sends is None:
            self.copy.start()
        else:
            pl.when(self.sends)(self.copy.start)

    def arrive(self):
        if self.gets is None:
            self.copy.wait_recv()
        else:
            pl.when(self.gets)(self.copy.wait_recv)

            @pl.when(jnp.logical_not(self.gets))
            def _():
                self.dst[...] = jnp.zeros_like(self.dst)

    def sent(self):
        if self.sends is None:
            self.copy.wait_send()
        else:
            pl.when(self.sends)(self.copy.wait_send)


def greet():
    barrier = pltpu.get_barrier_semaphore()
    gx, gxn = lax.axis_index("gx"), lax.axis_size("gx")
    gy, gyn = lax.axis_index("gy"), lax.axis_size("gy")
    ma, count = lax.axis_index("ma"), lax.axis_size("ma")
    for step in (1, gxn - 1):
        pl.semaphore_signal(
            barrier, inc=1, device_id={"gx": lax.rem(gx + step, gxn)}, device_id_type=MESH
        )
    for s in range(1, count):
        pl.semaphore_signal(
            barrier, inc=1, device_id={"ma": lax.rem(ma + s, count)}, device_id_type=MESH
        )
    for step, there in ((-1, gy > 0), (1, gy < gyn - 1)):

        @pl.when(there)
        def _(step=step):
            for s in range(count):
                pl.semaphore_signal(
                    barrier,
                    inc=1,
                    device_id={"gy": gy + step, "ma": lax.rem(ma + s, count)},
                    device_id_type=MESH,
                )

    below, above = jnp.minimum(gy, 1), jnp.minimum(gyn - 1 - gy, 1)
    pl.semaphore_wait(barrier, 2 + (count - 1) + (below + above) * count)


def core_kernel(
    widths, lat_i, lat_w, lon_i, lon_w, alpha, perts, innov, weight,
    increment, residual, p_north, p_south, p_west, p_east, lon_taps, lat_back,
    a_tile, p_tile, fine_tile, pick, edge_taps, lat_fore, v_strip, v_side, p_right, p_left,
    f_low, f_high, f_right, f_left, f_west, f_east, fine_wide,
    lat_i_low, lat_i_high, lat_w_low, lat_w_high, lon_i_west, lon_i_east, lon_w_west, lon_w_east,
    up_lon, up_lat, down_lat, down_lon, ext, other, low, high, to_east, to_west, from_west, from_east,
    send, recv, local,
):
    members, levels, rows, cols = alpha.shape
    steps, half, slots = members // GROUP, rows // 2, GROUP * HB
    frows, fcols = innov.shape[1:]
    fhalf = frows // 2
    ma, count = lax.axis_index("ma"), lax.axis_size("ma")
    loads = [
        pltpu.make_async_copy(src, dst, local.at[i])
        for i, (src, dst) in enumerate(
            (
                (perts, p_tile),
                (innov.at[ma], fine_tile.at[0]),
                (weight.at[ma], fine_tile.at[1]),
                (alpha, a_tile),
            )
        )
    ]
    for load in loads:
        load.start()
    counter = iter(range(96))
    pending = []

    def link(axis, step, src, dst, also=None):
        one = Link(axis, step, src, dst, send, recv, next(counter), also)
        pending.append(one)
        return one

    r, c = iota((cols, 2 * cols), 0), iota((cols, 2 * cols), 1)
    base = jnp.where(
        ((c < cols) & (r - (cols - HB) == c % HB)) | ((c >= cols) & (r == c % HB)), 1.0, 0.0
    )
    turned = (c % cols) // slots
    slot = jnp.where(c < cols, turned, 1 - turned) * GROUP + c % slots // HB
    for l in range(levels):
        for k in range(GROUP):
            at = slice(k % 2 * cols, (k % 2 + 1) * cols)
            n = l * GROUP + k
            pick[n // 2, at] = jnp.where(slot == n, base, 0.0).astype(BF16)
    greet()

    f_rows = [
        link("gy", 1, innov.at[ma, pl.ds(frows - FR, FR)], f_low.at[0]),
        link("gy", -1, innov.at[ma, pl.ds(0, FR)], f_high.at[0]),
        link("gy", 1, weight.at[ma, pl.ds(frows - FR, FR)], f_low.at[1]),
        link("gy", -1, weight.at[ma, pl.ds(0, FR)], f_high.at[1]),
    ]
    p_rows = [
        link("gy", 1, perts.at[:, :, pl.ds(rows - HB, HB), :], p_north),
        link("gy", -1, perts.at[:, :, pl.ds(0, HB), :], p_south),
    ]
    small = [
        link("gy", 1, lat_i, lat_i_low),
        link("gy", -1, lat_i, lat_i_high),
        link("gy", 1, lat_w, lat_w_low),
        link("gy", -1, lat_w, lat_w_high),
        link("gx", 1, lon_i, lon_i_west),
        link("gx", -1, lon_i, lon_i_east),
        link("gx", 1, lon_w, lon_w_west),
        link("gx", -1, lon_w, lon_w_east),
    ]
    for one in small + f_rows + p_rows:
        one.start()

    def f_edge(top, bottom, start):
        return lanes_of(*[part[i, :, start : start + FC] for part in (top, bottom) for i in range(2)])

    def f_sides(span):
        pair = [
            link("gx", 1, f_right.at[span], f_west.at[span]),
            link("gx", -1, f_left.at[span], f_east.at[span]),
        ]
        for one in pair:
            one.start()
        return pair

    for load in loads[1:3]:
        load.wait()
    for dst, start in ((f_right, fcols - FC), (f_left, 0)):
        dst[:fhalf] = f_edge(fine_tile.at[:, :fhalf], fine_tile.at[:, fhalf:], start)
    f_arrive = f_sides(pl.ds(0, fhalf))

    def packed(piece):
        total = None
        for l in range(levels):
            for k in range(0, GROUP, 2):
                n = (l * GROUP + k) // 2
                part = dot(lanes_of(piece(l, k), piece(l, k + 1)), pick[n])
                total = part if total is None else total + part
        return total.astype(BF16)

    loads[0].wait()
    p_arrive = []
    for g in range(steps):
        both = packed(lambda l, k: p_tile[g * GROUP + k, l])
        p_right[g, :rows] = both[:, :cols]
        p_left[g, :rows] = both[:, cols:]
        span = pl.ds(0, rows)
        pair = [
            link("gx", 1, p_right.at[g, span], p_west.at[g, span]),
            link("gx", -1, p_left.at[g, span], p_east.at[g, span]),
        ]
        for one in pair:
            one.start()
        p_arrive += pair

    lane = iota((cols, cols), 1)
    deep = half + 2 * HB
    wide_k = lat_fore.shape[3]
    for l in range(levels):
        spread = widths[l].astype(F32)
        scale = tap_scale(spread)
        cell, at = iota((cols, cols), 0), lane
        lon_taps[l, 0], lon_taps[l, 1] = split(tap_value(cell - at, spread, scale))
        lon_taps[l, 2], lon_taps[l, 3] = split(tap_value(side_cell(cell, l, cols) - at, spread, scale))
        edge_taps[l, 0], edge_taps[l, 1] = split(tap_value(side_cell(at, l, cols) - cell, spread, scale))
        lat_back[l] = lat_taps(spread, scale, half, deep, -HB, wide_k)
        lat_fore[l, 0] = lat_taps(spread, scale, deep, deep, HB, wide_k)
        lat_fore[l, 1] = lat_taps(spread, scale, deep, deep, -2 * HB, wide_k)
    loads[3].wait()

    def tall(u, l):
        h, lo = split(u)
        out = []
        for b in range(2):
            at = slice(b * (rows - deep), b * (rows - deep) + deep)
            stack = rows_of(h[at], h[at], lo[at])
            out.append(dot(lat_fore[l, b, :, : 3 * deep], stack)[: half + HB])
        return out

    for l in range(levels):
        ext[l, HB : HB + rows, :cols] = jnp.zeros((rows, cols), F32)

    @pl.loop(0, steps)
    def _(g):
        for l in range(levels):
            taps = rows_of(
                lanes_of(lon_taps[l, 0], edge_taps[l, 0]), lanes_of(lon_taps[l, 1], edge_taps[l, 1])
            )
            side = total = None
            for k in range(0, GROUP, 2):
                cores = []
                for m in (k, k + 1):
                    a = a_tile[g * GROUP + m, l]
                    u = dot(lanes_of(a, a), taps)
                    cores.append(u[:, :cols])
                    mine = lane % slots // HB == m
                    side = u[:, cols:] if side is None else jnp.where(mine, u[:, cols:], side)
                top, bottom = tall(lanes_of(*cores), l)
                for i, m in enumerate((k, k + 1)):
                    at = slice(i * cols, (i + 1) * cols)
                    v = rows_of(top[HB:, at], bottom[:half, at])
                    part = p_tile[g * GROUP + m, l].astype(F32) * v
                    total = part if total is None else total + part
                    v_strip[g * GROUP + m, l] = rows_of(top[:HB, at], bottom[half:, at])
            ext[l, HB : HB + rows, :cols] += total
            v_side[g, l] = rows_of(*tall(side, l))

    for one in p_rows:
        one.arrive()

    both = packed(
        lambda l, k: rows_of(
            *[
                part[g * GROUP + k, l].astype(F32)
                for g in range(steps)
                for part in (p_north, p_south)
            ]
        ).astype(BF16)
    )
    for g in range(steps):
        at = slice(2 * HB * g, 2 * HB * (g + 1))
        p_right[g, rows:] = both[at, :cols]
        p_left[g, rows:] = both[at, cols:]
    span = pl.ds(rows, 2 * HB)
    corners = [
        link("gx", 1, p_right.at[:, span], p_west.at[:, span]),
        link("gx", -1, p_left.at[:, span], p_east.at[:, span]),
    ]
    for one in corners:
        one.start()
    p_arrive += corners
    for one in f_rows:
        one.arrive()
    for dst, start in ((f_right, fcols - FC), (f_left, 0)):
        dst[fhalf:] = f_edge(f_low, f_high, start)
    f_arrive += f_sides(pl.ds(fhalf, FR))

    for one in small:
        one.arrive()
    lat_at = lanes_of(lat_i[...], lat_i_low[:, frows - FR :], lat_i_high[:, :FR]).astype(F32)
    lat_by = lanes_of(lat_w[...], lat_w_low[:, frows - FR :], lat_w_high[:, :FR])
    lat_at = lat_at - (lax.axis_index("gy") * rows).astype(F32)
    lon_at = lanes_of(lon_i[...], lon_i_west[:, fcols - FC :], lon_i_east[:, :FC]).astype(F32)
    lon_by = lanes_of(lon_w[...], lon_w_west[:, fcols - FC :], lon_w_east[:, :FC])
    lon_total = float(cols * lax.axis_size("gx"))
    lon_at = lon_at - (lax.axis_index("gx") * cols).astype(F32)
    lon_at = jnp.where(
        lon_at < -64.0, lon_at + lon_total, jnp.where(lon_at >= lon_total - 64.0, lon_at - lon_total, lon_at)
    )
    f_tall, f_wide = frows + 2 * FR, fcols + 2 * FC

    def upright(at, by):
        size = at.shape[1]
        space = jnp.zeros((1, -size % 128), F32)
        at, by = lanes_of(at, space), lanes_of(by, space)
        shape = (8, at.shape[1])
        both = jnp.where(iota(shape, 0) == 0, jnp.broadcast_to(at, shape), jnp.broadcast_to(by, shape))
        both = both.T[:size]
        return both[:, 0:1], both[:, 1:2]

    lat_at_up, lat_by_up = upright(lat_at, lat_by)
    lon_at_up, lon_by_up = upright(lon_at, lon_by)
    t_rows, e_rows = rows + 2 * CR, rows + 2 * HB
    up_lat[0], up_lat[1] = split(weigh(iota((f_tall, t_rows), 1) - CR, lat_at_up, lat_by_up))
    down_lat[0], down_lat[1] = split(weigh(iota((e_rows, f_tall), 0) - HB, lat_at, lat_by))
    order = iota((2 * cols, f_wide), 0)
    w = order - cols
    wing = jnp.where(
        w < REACH,
        w - (REACH - HB),
        jnp.where(
            (w >= slots - HB) & (w < slots),
            w - slots,
            jnp.where(
                (w >= slots) & (w < slots + REACH),
                w - slots + cols - HB,
                jnp.where(w >= cols - HB, w + HB, -1000),
            ),
        ),
    )
    up_lon[0], up_lon[1] = split(weigh(jnp.where(w < 0, order, wing), lon_at, lon_by))
    order = iota((f_wide, 2 * cols), 1)
    cell = jnp.where(order < cols, order, side_cell(order - cols, ma, cols))
    down_lon[0], down_lon[1] = split(weigh(cell, lon_at_up, lon_by_up))

    for l in range(levels):

        def strips(g, sums):
            north, south = sums
            for k in range(GROUP):
                m = g * GROUP + k
                north = north + p_north[m, l].astype(F32) * v_strip[m, l, :HB]
                south = south + p_south[m, l].astype(F32) * v_strip[m, l, HB:]
            return north, south

        zero = jnp.zeros((HB, cols), F32)
        north, south = lax.fori_loop(0, steps, strips, (zero, zero))
        ext[l, :HB, :cols] = north
        ext[l, HB + rows :, :cols] = south

    for one in f_arrive:
        one.arrive()
    for i in range(2):

        def wing_of(part):
            x, y = FC * i, 2 * FC + FC * i
            return rows_of(
                part[:fhalf, x : x + FC],
                part[:fhalf, y : y + FC],
                part[fhalf:, x : x + FC],
                part[fhalf:, y : y + FC],
            )

        fine_wide[i] = lanes_of(
            rows_of(fine_tile[i], f_low[i], f_high[i]), wing_of(f_west), wing_of(f_east)
        )

    for one in p_arrive:
        one.arrive()
    tall_lane = iota((e_rows, cols), 1)
    for l in range(levels):
        total = None
        for g in range(steps):
            side = jnp.where(
                tall_lane // slots == l, p_west[g].astype(F32), p_east[g].astype(F32)
            )
            part = natural(side, rows) * v_side[g, l]
            total = part if total is None else total + part
        ext[l, :, cols:] = total if l == 0 else pltpu.roll(total, slots, 1)

    swaps, lows, highs = [], [], []
    for s in range(count):
        peer = lax.rem(ma + s, count)
        if s:
            swaps.append(link("ma", peer - ma, ext.at[peer], other.at[s - 1]))
        lows.append(link("gy", 1, ext.at[peer, pl.ds(e_rows - STRIP, STRIP)], low.at[s], peer))
        highs.append(link("gy", -1, ext.at[peer, pl.ds(0, STRIP)], high.at[s], peer))
    for one in lows + highs + swaps:
        one.start()
    for one in swaps + lows + highs:
        one.arrive()
    mine = ext[ma]
    for s in range(count - 1):
        mine = mine + other[s]
    above, below = low[0], high[0]
    for s in range(1, count):
        above, below = above + low[s], below + high[s]
    lap = CR - HB
    edge = STRIP - lap
    mine = rows_of(
        above[:lap],
        mine[:edge] + above[lap:],
        mine[edge : e_rows - edge],
        mine[e_rows - edge :] + below[:edge],
        below[edge:],
    )
    core, side = mine[:, :cols], mine[:, cols:]
    for shift in (HB, 2 * HB, 4 * HB):
        side = side + pltpu.roll(side, shift, 1)

    blocks = (t_rows + STRIP - 1) // STRIP
    t_lane = iota((t_rows, cols), 1)
    thin = iota((STRIP, cols), 1)

    def fold(x, first):
        if blocks * STRIP > t_rows:
            x = rows_of(x, jnp.zeros((blocks * STRIP - t_rows, cols), F32))
        total = None
        for b in range(blocks):
            part = pltpu.roll(x[b * STRIP : (b + 1) * STRIP], (b * REACH - first) % cols, 1)
            total = part if total is None else jnp.where(thin >= b * REACH, part, total)
        return total

    def unfold(x, first):
        parts = [pltpu.roll(x, (first - b * REACH) % cols, 1) for b in range(blocks)]
        return rows_of(*parts)[:t_rows]

    eastward = jnp.where(t_lane >= cols - HB, side, pltpu.roll(core, cols - HB, 1))
    westward = jnp.where(t_lane < slots, side, pltpu.roll(core, slots, 1))
    to_east[...] = fold(eastward, cols - REACH)
    to_west[...] = fold(westward, slots - HB)
    sides = [
        link("gx", 1, to_east, from_west),
        link("gx", -1, to_west, from_east),
    ]
    for one in sides:
        one.start()
    for one in sides:
        one.arrive()
    wings = jnp.where(
        t_lane < REACH,
        unfold(from_west[...], 0),
        jnp.where((t_lane >= slots) & (t_lane < slots + REACH), unfold(from_east[...], slots), side),
    )
    across = dot3(split(lanes_of(core, wings)), (up_lon[0], up_lon[1]))
    fine = dot3((up_lat[0], up_lat[1]), split(across))
    increment[ma] = fine[:frows, :fcols]
    misfit = fine_wide[1] * (fine - fine_wide[0])
    across = dot3((down_lat[0], down_lat[1]), split(misfit))
    residual[ma] = dot3(split(across), (down_lon[0], down_lon[1]))
    ends = []
    for s in range(1, count):
        peer = lax.rem(ma + s, count)
        for whole in (residual, increment):
            ends.append(link("ma", peer - ma, whole.at[ma], whole.at[ma]))
    for one in ends:
        one.start()
    for one in ends:
        one.arrive()
    for one in pending:
        one.sent()


def cost(flops, nbytes):
    return pl.CostEstimate(flops=flops, bytes_accessed=nbytes, transcendentals=0)


def core_step(widths, lat_i, lat_w, lon_i, lon_w, alpha, perts, innov, weight):
    members, levels, rows, cols = alpha.shape
    steps = members // GROUP
    frows, fcols = innov.shape[1:]
    count = lax.axis_size("ma")
    assert levels == 2 and count == levels
    half = rows // 2
    deep = half + 2 * HB
    wide_k = -(-3 * deep // 128) * 128
    e_rows, t_rows = rows + 2 * HB, rows + 2 * CR
    f_tall, f_wide = frows + 2 * FR, fcols + 2 * FC
    strip = ((members, levels, HB, cols), BF16)
    side = ((steps, e_rows, cols), BF16)
    outs = [
        (innov.shape, F32),
        ((levels, e_rows, 2 * cols), F32),
        strip,
        strip,
        side,
        side,
        ((levels, 4, cols, cols), BF16),
        ((levels, half, wide_k), BF16),
    ]
    fine_edge = ((2, FR, fcols), F32)
    fine_side = ((frows // 2 + FR, 4 * FC), F32)
    scratch = [
        (alpha.shape, BF16),
        (alpha.shape, BF16),
        ((2, frows, fcols), F32),
        ((levels * GROUP // 2, 2 * cols, 2 * cols), BF16),
        ((levels, 2, cols, cols), BF16),
        ((levels, 2, deep, wide_k), BF16),
        ((members, levels, 2 * HB, cols), F32),
        ((steps, levels, e_rows, cols), F32),
        side,
        side,
        fine_edge,
        fine_edge,
        fine_side,
        fine_side,
        fine_side,
        fine_side,
        ((2, f_tall, f_wide), F32),
        (lat_i.shape, jnp.int32),
        (lat_i.shape, jnp.int32),
        (lat_w.shape, F32),
        (lat_w.shape, F32),
        (lon_i.shape, jnp.int32),
        (lon_i.shape, jnp.int32),
        (lon_w.shape, F32),
        (lon_w.shape, F32),
        ((2, 2 * cols, f_wide), BF16),
        ((2, f_tall, t_rows), BF16),
        ((2, e_rows, f_tall), BF16),
        ((2, f_wide, 2 * cols), BF16),
        ((levels, e_rows, 2 * cols), F32),
        ((count - 1, e_rows, 2 * cols), F32),
        ((count, STRIP, 2 * cols), F32),
        ((count, STRIP, 2 * cols), F32),
    ] + [((STRIP, cols), F32)] * 4
    vmem = pl.BlockSpec(memory_space=pltpu.VMEM)
    anywhere = pl.BlockSpec(memory_space=pl.ANY)
    return pl.pallas_call(
        core_kernel,
        in_specs=[pl.BlockSpec(memory_space=pltpu.SMEM)] + [vmem] * 4 + [anywhere] * 4,
        out_specs=[vmem] * len(outs),
        out_shape=[jax.ShapeDtypeStruct(shape, kind) for shape, kind in outs],
        scratch_shapes=[pltpu.VMEM(shape, kind) for shape, kind in scratch]
        + [
            pltpu.SemaphoreType.DMA((96,)),
            pltpu.SemaphoreType.DMA((96,)),
            pltpu.SemaphoreType.DMA((4,)),
        ],
        compiler_params=pltpu.CompilerParams(
            collective_id=0, has_side_effects=True, vmem_limit_bytes=VMEM_LIMIT
        ),
        cost_estimate=cost(2**30, 2**24),
    )(widths, lat_i, lat_w, lon_i, lon_w, alpha, perts, innov, weight)


def band(high, low, taps):
    half = taps.shape[0]
    deep = half + 2 * HB
    out = []
    for first in range(0, high.shape[0] - 2 * HB, half):
        h, lo = high[first : first + deep], low[first : first + deep]
        out.append(dot(taps, rows_of(h, h, lo)))
    return rows_of(*out)


def adjoint_kernel(alpha, perts, north, south, west, east, residual, lon, lat, out):
    rows, cols = alpha.shape[2:]
    slots = GROUP * HB
    l = pl.program_id(1)
    res = residual[l]
    wide = iota((rows + 2 * HB, cols), 1)
    side = jnp.where(wide // slots == l, west[0].astype(F32), east[0].astype(F32))
    side = natural(side, rows) * res[:, cols:]
    taps = lat[l, :, : 3 * (rows // 2 + 2 * HB)]
    zero = jnp.zeros((cols, cols), BF16)

    def stack(high, low):
        return rows_of(lanes_of(high, low), lanes_of(high, zero))

    core, wing = stack(lon[l, 0], lon[l, 1]), stack(lon[l, 2], lon[l, 3])
    edge_h, edge_l = split(band(*split(side), taps))
    lane = iota((rows, cols), 1)
    for k in range(0, GROUP, 2):
        pairs = []
        for m in (k, k + 1):
            tall = rows_of(north[m, 0].astype(F32), perts[m, 0].astype(F32), south[m, 0].astype(F32))
            pairs.append(split(tall * res[:, :cols]))
        both = band(lanes_of(pairs[0][0], pairs[1][0]), lanes_of(pairs[0][1], pairs[1][1]), taps)
        for i, m in enumerate((k, k + 1)):
            mine = lane % slots // HB == m
            edges = lanes_of(
                jnp.where(mine, edge_h, jnp.zeros_like(edge_h)),
                jnp.where(mine, edge_l, jnp.zeros_like(edge_l)),
            )
            total = dot(lanes_of(*split(both[:, i * cols : (i + 1) * cols])), core) + dot(edges, wing)
            out[m, 0] = alpha[m, 0].astype(F32) + (total[:, :cols] + total[:, cols:])


def adjoint(alpha, perts, north, south, west, east, residual, lon, lat):
    members, levels, rows, cols = alpha.shape
    block = pl.BlockSpec((GROUP, 1, rows, cols), lambda g, l: (g, l, 0, 0))
    strip = pl.BlockSpec((GROUP, 1, HB, cols), lambda g, l: (g, l, 0, 0))
    side = pl.BlockSpec((1, rows + 2 * HB, cols), lambda g, l: (g, 0, 0))

    def whole(x):
        return pl.BlockSpec(x.shape, lambda g, l: (0,) * x.ndim)

    return pl.pallas_call(
        adjoint_kernel,
        grid=(members // GROUP, levels),
        in_specs=[block, block, strip, strip, side, side, whole(residual), whole(lon), whole(lat)],
        out_specs=block,
        out_shape=jax.ShapeDtypeStruct(alpha.shape, F32),
        cost_estimate=cost(members * levels * 2**25, alpha.size * 8),
    )(alpha, perts, north, south, west, east, residual, lon, lat)


def body(
    alpha_fields,
    member_perts,
    band_widths,
    lat_index,
    lat_weight,
    lon_index,
    lon_weight,
    innovation,
    obs_weight,
):
    tables = [x.reshape(1, -1) for x in (lat_index, lat_weight, lon_index, lon_weight)]
    increment, residual, *halos = core_step(
        band_widths, *tables, alpha_fields, member_perts, innovation, obs_weight
    )
    north, south, west, east, lon, lat = halos
    gradient = adjoint(alpha_fields, member_perts, north, south, west, east, residual, lon, lat)
    return (increment, gradient)


def solution(mesh):
    placed = (
        P("ma", None, "gy", "gx"),
        P("ma", None, "gy", "gx"),
        P(),
        P("gy"),
        P("gy"),
        P("gx"),
        P("gx"),
        P(None, "gy", "gx"),
        P(None, "gy", "gx"),
    )
    return jax.shard_map(
        body,
        mesh=mesh,
        in_specs=placed,
        out_specs=(P(None, "gy", "gx"), P("ma", None, "gy", "gx")),
        check_vma=False,
    )
```

profile of v0, /device:TPU:0, one launch (start us, length us, event | category | flops | bytes accessed | tf_op | source)
XLA Modules:
  0.0 48.5 jit_solution(10968514439836600334)
XLA Ops:
  0.6 34.2 %shard_map.104 = (f32[2,256,256]{2,1,0:T(8,128)}, f32[2,144,256]{2,1,0:T(8,128)}, bf16[40,2,8,128]{3,2,1,0:T(8,128)(2,1)}, bf16[40,2,8,128]{3,2,1,0:T(8,128)(2,1...) custom-call(s32[2]{0:T(128)} %widths.1, ...), custom_call_target="tpu_custom_call" | custom-call | flops 1073741824 | bytes 16777216 | tf_op jit(solution)/shard_map/pallas_call | solution.py:595
  34.9 0.0 copy-start
  34.9 12.9 %shard_map.105 = f32[40,2,128,128]{3,2,1,0:T(8,128)} custom-call(bf16[40,2,128,128]{3,2,1,0:T(8,128)(2,1)} %alpha.3, bf16[40,2,128,128]{3,2,1,0:T(8,128)(2,1)} %perts.3, bf16[40,2,8,128]{3,2,1,0:T(8,128)(2,1)} %get-tuple-element.11.north, bf16[40,2,8,128]{3,2,1,0:T(8,128)(2,1)} %get-tuple-element.12.south, bf16[5,144,128]{2,1,0:T(8,128)(2,1)} %get-tuple-element.13.west, ...), custom_call_target="tpu_custom_call" | custom-call | flops 2684354560 | bytes 10485760 | tf_op jit(solution)/shard_map/pallas_call | solution.py:665
  47.7 0.0 copy-done
  47.8 0.8 %copy.12 = f32[2,256,256]{2,1,0:T(8,128)} copy(f32[2,256,256]{2,1,0:T(8,128)S(1)} %copy-done) | data formatting | bytes 1048576
Async XLA Ops:
  34.9 12.9 %copy-start = (f32[2,256,256]{2,1,0:T(8,128)S(1)}, f32[2,256,256]{2,1,0:T(8,128)}, u32[]{:S(2)}) copy-start(f32[2,256,256]{2,1,0:T(8,128)} %get-tuple-element.20) | copy-start | bytes 1572868
where the time goes:
time: 48.9 us; the launch traced here: 48.5 us
  Pallas kernels  47.1 us (96%)
  local copies, waits for them, and re-layouts  0.8 us (2%)
  between operations  0.65 us (1%)
    pallas_call x1, Pallas kernels, core_step(): pl.pallas_call(core_kernel, in_specs=[pl.BlockSpec(memory_space=pltpu.SME...  34.2 us
    pallas_call x1, Pallas kernels, adjoint(): pl.pallas_call(adjoint_kernel, grid=(members // GROUP, levels), in_specs=...  12.9 us

commit v1 on v0

--- a/solution.py
+++ b/solution.py
@@ -8,7 +8,8 @@
 HB = 8
 GROUP = 8
 FR = 24
-FC = 32
+FC = 20
+FOLD = 3
 CR = 16
 STRIP = 24
 REACH = HB + 10
@@ -93,7 +94,7 @@
             self.sends = (target >= 0) & (target < count)
             self.gets = (me - step >= 0) & (me - step < count)
         self.dst = dst
-        device = {axis: target} if also is None else {axis: target, "ma": also}
+        device = {axis: target, **(also or {})}
         self.copy = pltpu.make_async_remote_copy(
             src_ref=src,
             dst_ref=dst,
@@ -150,9 +151,16 @@
                     device_id={"gy": gy + step, "ma": lax.rem(ma + s, count)},
                     device_id_type=MESH,
                 )
+            for side in (1, gxn - 1):
+                pl.semaphore_signal(
+                    barrier,
+                    inc=1,
+                    device_id={"gx": lax.rem(gx + side, gxn), "gy": gy + step},
+                    device_id_type=MESH,
+                )
 
     below, above = jnp.minimum(gy, 1), jnp.minimum(gyn - 1 - gy, 1)
-    pl.semaphore_wait(barrier, 2 + (count - 1) + (below + above) * count)
+    pl.semaphore_wait(barrier, 2 + (count - 1) + (below + above) * (count + 2))
 
 
 def core_kernel(
@@ -167,20 +175,19 @@
     members, levels, rows, cols = alpha.shape
     steps, half, slots = members // GROUP, rows // 2, GROUP * HB
     frows, fcols = innov.shape[1:]
-    fhalf = frows // 2
     ma, count = lax.axis_index("ma"), lax.axis_size("ma")
-    loads = [
-        pltpu.make_async_copy(src, dst, local.at[i])
-        for i, (src, dst) in enumerate(
-            (
-                (perts, p_tile),
-                (innov.at[ma], fine_tile.at[0]),
-                (weight.at[ma], fine_tile.at[1]),
-                (alpha, a_tile),
-            )
-        )
+    gx, gxn = lax.axis_index("gx"), lax.axis_size("gx")
+    f_loads = [
+        pltpu.make_async_copy(src.at[ma], fine_tile.at[i], local.at[i])
+        for i, src in enumerate((innov, weight))
     ]
-    for load in loads:
+
+    def group_load(src, dst, g, first):
+        span = pl.ds(g * GROUP, GROUP)
+        return pltpu.make_async_copy(src.at[span], dst.at[span], local.at[first + g])
+
+    p_loads = [group_load(perts, p_tile, g, 2) for g in range(steps)]
+    for load in f_loads + p_loads:
         load.start()
     counter = iter(range(96))
     pending = []
@@ -226,23 +233,50 @@
     for one in small + f_rows + p_rows:
         one.start()
 
-    def f_edge(top, bottom, start):
-        return lanes_of(*[part[i, :, start : start + FC] for part in (top, bottom) for i in range(2)])
-
-    def f_sides(span):
-        pair = [
-            link("gx", 1, f_right.at[span], f_west.at[span]),
-            link("gx", -1, f_left.at[span], f_east.at[span]),
-        ]
-        for one in pair:
-            one.start()
-        return pair
-
-    for load in loads[1:3]:
+    def tilted(src, dst, side, top, bottom, first):
+        pairs = []
+        for step, at, to in ((1, bottom, first), (-1, top, first + HB)):
+            span, there = pl.ds(at, HB), pl.ds(to, HB)
+            index = (slice(None),) * (src.ndim - 2)
+            pairs.append(
+                link(
+                    "gy",
+                    step,
+                    src.at[(*index, span)],
+                    dst.at[(*index, there)],
+                    {"gx": lax.rem(gx + side, gxn)},
+                )
+            )
+        return pairs
+
+    f_main = f_west.shape[0] - 2 * HB
+
+    def f_fold(first, count, start):
+        deep = -(-count // (FOLD * HB)) * HB
+        parts = []
+        for b in range(FOLD):
+            stop = min(first + (b + 1) * deep, first + count)
+            for i in range(2):
+                part = fine_tile[i, first + b * deep : stop, start : start + FC]
+                short = deep - part.shape[0]
+                parts.append(rows_of(part, jnp.zeros((short, FC), F32)) if short else part)
+        return lanes_of(*parts, jnp.zeros((deep, cols - 2 * FOLD * FC), F32))
+
+    for load in f_loads:
         load.wait()
-    for dst, start in ((f_right, fcols - FC), (f_left, 0)):
-        dst[:fhalf] = f_edge(fine_tile.at[:, :fhalf], fine_tile.at[:, fhalf:], start)
-    f_arrive = f_sides(pl.ds(0, fhalf))
+    f_arrive = []
+    for step, side, src, dst, start in (
+        (1, 1, f_right, f_west, fcols - FC),
+        (-1, gxn - 1, f_left, f_east, 0),
+    ):
+        src[:f_main] = f_fold(0, frows, start)
+        src[f_main : f_main + HB] = f_fold(0, FR, start)
+        src[f_main + HB :] = f_fold(frows - FR, FR, start)
+        span = pl.ds(0, f_main)
+        f_arrive.append(link("gx", step, src.at[span], dst.at[span]))
+        f_arrive += tilted(src, dst, side, f_main, f_main + HB, f_main)
+    for one in f_arrive:
+        one.start()
 
     def packed(piece):
         total = None
@@ -253,20 +287,27 @@
                 total = part if total is None else total + part
         return total.astype(BF16)
 
-    loads[0].wait()
+    a_loads = [group_load(alpha, a_tile, g, 2 + steps) for g in range(steps)]
     p_arrive = []
     for g in range(steps):
+        p_loads[g].wait()
+        a_loads[g].start()
         both = packed(lambda l, k: p_tile[g * GROUP + k, l])
-        p_right[g, :rows] = both[:, :cols]
-        p_left[g, :rows] = both[:, cols:]
+        p_right[g] = both[:, :cols]
+        p_left[g] = both[:, cols:]
         span = pl.ds(0, rows)
         pair = [
-            link("gx", 1, p_right.at[g, span], p_west.at[g, span]),
-            link("gx", -1, p_left.at[g, span], p_east.at[g, span]),
+            link("gx", 1, p_right.at[g], p_west.at[g, span]),
+            link("gx", -1, p_left.at[g], p_east.at[g, span]),
         ]
         for one in pair:
             one.start()
         p_arrive += pair
+    corners = tilted(p_right, p_west, 1, 0, rows - HB, rows)
+    corners += tilted(p_left, p_east, gxn - 1, 0, rows - HB, rows)
+    for one in corners:
+        one.start()
+    p_arrive += corners
 
     lane = iota((cols, cols), 1)
     deep = half + 2 * HB
@@ -281,7 +322,6 @@
         lat_back[l] = lat_taps(spread, scale, half, deep, -HB, wide_k)
         lat_fore[l, 0] = lat_taps(spread, scale, deep, deep, HB, wide_k)
         lat_fore[l, 1] = lat_taps(spread, scale, deep, deep, -2 * HB, wide_k)
-    loads[3].wait()
 
     def tall(u, l):
         h, lo = split(u)
@@ -297,6 +337,7 @@
 
     @pl.loop(0, steps)
     def _(g):
+        group_load(alpha, a_tile, g, 2 + steps).wait()
         for l in range(levels):
             taps = rows_of(
                 lanes_of(lon_taps[l, 0], edge_taps[l, 0]), lanes_of(lon_taps[l, 1], edge_taps[l, 1])
@@ -323,33 +364,8 @@
     for one in p_rows:
         one.arrive()
 
-    both = packed(
-        lambda l, k: rows_of(
-            *[
-                part[g * GROUP + k, l].astype(F32)
-                for g in range(steps)
-                for part in (p_north, p_south)
-            ]
-        ).astype(BF16)
-    )
-    for g in range(steps):
-        at = slice(2 * HB * g, 2 * HB * (g + 1))
-        p_right[g, rows:] = both[at, :cols]
-        p_left[g, rows:] = both[at, cols:]
-    span = pl.ds(rows, 2 * HB)
-    corners = [
-        link("gx", 1, p_right.at[:, span], p_west.at[:, span]),
-        link("gx", -1, p_left.at[:, span], p_east.at[:, span]),
-    ]
-    for one in corners:
-        one.start()
-    p_arrive += corners
     for one in f_rows:
         one.arrive()
-    for dst, start in ((f_right, fcols - FC), (f_left, 0)):
-        dst[fhalf:] = f_edge(f_low, f_high, start)
-    f_arrive += f_sides(pl.ds(fhalf, FR))
-
     for one in small:
         one.arrive()
     lat_at = lanes_of(lat_i[...], lat_i_low[:, frows - FR :], lat_i_high[:, :FR]).astype(F32)
@@ -418,12 +434,13 @@
     for i in range(2):
 
         def wing_of(part):
-            x, y = FC * i, 2 * FC + FC * i
+            def opened(first, last):
+                lanes = range(FC * i, 2 * FOLD * FC, 2 * FC)
+                return [part[first:last, x : x + FC] for x in lanes]
+
+            low, high = f_main, f_main + HB
             return rows_of(
-                part[:fhalf, x : x + FC],
-                part[:fhalf, y : y + FC],
-                part[fhalf:, x : x + FC],
-                part[fhalf:, y : y + FC],
+                rows_of(*opened(0, low))[:frows], *opened(low, high), *opened(high, high + HB)
             )
 
         fine_wide[i] = lanes_of(
@@ -448,8 +465,8 @@
         peer = lax.rem(ma + s, count)
         if s:
             swaps.append(link("ma", peer - ma, ext.at[peer], other.at[s - 1]))
-        lows.append(link("gy", 1, ext.at[peer, pl.ds(e_rows - STRIP, STRIP)], low.at[s], peer))
-        highs.append(link("gy", -1, ext.at[peer, pl.ds(0, STRIP)], high.at[s], peer))
+        lows.append(link("gy", 1, ext.at[peer, pl.ds(e_rows - STRIP, STRIP)], low.at[s], {"ma": peer}))
+        highs.append(link("gy", -1, ext.at[peer, pl.ds(0, STRIP)], high.at[s], {"ma": peer}))
     for one in lows + highs + swaps:
         one.start()
     for one in swaps + lows + highs:
@@ -510,16 +527,19 @@
     across = dot3(split(lanes_of(core, wings)), (up_lon[0], up_lon[1]))
     fine = dot3((up_lat[0], up_lat[1]), split(across))
     increment[ma] = fine[:frows, :fcols]
+    ends = []
+
+    def share(whole):
+        for s in range(1, count):
+            peer = lax.rem(ma + s, count)
+            ends.append(link("ma", peer - ma, whole.at[ma], whole.at[ma]))
+            ends[-1].start()
+
+    share(increment)
     misfit = fine_wide[1] * (fine - fine_wide[0])
     across = dot3((down_lat[0], down_lat[1]), split(misfit))
     residual[ma] = dot3(split(across), (down_lon[0], down_lon[1]))
-    ends = []
-    for s in range(1, count):
-        peer = lax.rem(ma + s, count)
-        for whole in (residual, increment):
-            ends.append(link("ma", peer - ma, whole.at[ma], whole.at[ma]))
-    for one in ends:
-        one.start()
+    share(residual)
     for one in ends:
         one.arrive()
     for one in pending:
@@ -554,7 +574,8 @@
         ((levels, half, wide_k), BF16),
     ]
     fine_edge = ((2, FR, fcols), F32)
-    fine_side = ((frows // 2 + FR, 4 * FC), F32)
+    fine_side = ((-(-frows // (FOLD * HB)) * HB + 2 * HB, cols), F32)
+    packed = ((steps, rows, cols), BF16)
     scratch = [
         (alpha.shape, BF16),
         (alpha.shape, BF16),
@@ -564,8 +585,8 @@
         ((levels, 2, deep, wide_k), BF16),
         ((members, levels, 2 * HB, cols), F32),
         ((steps, levels, e_rows, cols), F32),
-        side,
-        side,
+        packed,
+        packed,
         fine_edge,
         fine_edge,
         fine_side,
@@ -601,7 +622,7 @@
         + [
             pltpu.SemaphoreType.DMA((96,)),
             pltpu.SemaphoreType.DMA((96,)),
-            pltpu.SemaphoreType.DMA((4,)),
+            pltpu.SemaphoreType.DMA((2 + 2 * steps,)),
         ],
         compiler_params=pltpu.CompilerParams(
             collective_id=0, has_side_effects=True, vmem_limit_bytes=VMEM_LIMIT
@@ -620,10 +641,28 @@
     return rows_of(*out)
 
 
-def adjoint_kernel(alpha, perts, north, south, west, east, residual, lon, lat, out):
+def adjoint_kernel(
+    alpha, perts, north, south, west, east, residual, lon, lat, fine, out, fine_out, held, sems
+):
     rows, cols = alpha.shape[2:]
     slots = GROUP * HB
-    l = pl.program_id(1)
+    g, l = pl.program_id(0), pl.program_id(1)
+    take = pltpu.make_async_copy(fine, held, sems.at[0])
+    give = pltpu.make_async_copy(held, fine_out, sems.at[1])
+
+    @pl.when((g == 0) & (l == 0))
+    def _():
+        take.start()
+
+    @pl.when((g == 1) & (l == 0))
+    def _():
+        take.wait()
+        give.start()
+
+    @pl.when((g == pl.num_programs(0) - 1) & (l == pl.num_programs(1) - 1))
+    def _():
+        give.wait()
+
     res = residual[l]
     wide = iota((rows + 2 * HB, cols), 1)
     side = jnp.where(wide // slots == l, west[0].astype(F32), east[0].astype(F32))
@@ -653,7 +692,7 @@
             out[m, 0] = alpha[m, 0].astype(F32) + (total[:, :cols] + total[:, cols:])
 
 
-def adjoint(alpha, perts, north, south, west, east, residual, lon, lat):
+def adjoint(alpha, perts, north, south, west, east, residual, lon, lat, fine):
     members, levels, rows, cols = alpha.shape
     block = pl.BlockSpec((GROUP, 1, rows, cols), lambda g, l: (g, l, 0, 0))
     strip = pl.BlockSpec((GROUP, 1, HB, cols), lambda g, l: (g, l, 0, 0))
@@ -665,11 +704,16 @@
     return pl.pallas_call(
         adjoint_kernel,
         grid=(members // GROUP, levels),
-        in_specs=[block, block, strip, strip, side, side, whole(residual), whole(lon), whole(lat)],
-        out_specs=block,
-        out_shape=jax.ShapeDtypeStruct(alpha.shape, F32),
+        in_specs=[block, block, strip, strip, side, side, whole(residual), whole(lon), whole(lat)]
+        + [pl.BlockSpec(memory_space=pl.ANY)],
+        out_specs=[block, pl.BlockSpec(memory_space=pl.ANY)],
+        out_shape=[
+            jax.ShapeDtypeStruct(alpha.shape, F32),
+            jax.ShapeDtypeStruct(fine.shape, F32),
+        ],
+        scratch_shapes=[pltpu.VMEM(fine.shape, F32), pltpu.SemaphoreType.DMA((2,))],
         cost_estimate=cost(members * levels * 2**25, alpha.size * 8),
-    )(alpha, perts, north, south, west, east, residual, lon, lat)
+    )(alpha, perts, north, south, west, east, residual, lon, lat, fine)
 
 
 def body(
@@ -688,7 +732,9 @@
         band_widths, *tables, alpha_fields, member_perts, innovation, obs_weight
     )
     north, south, west, east, lon, lat = halos
-    gradient = adjoint(alpha_fields, member_perts, north, south, west, east, residual, lon, lat)
+    gradient, increment = adjoint(
+        alpha_fields, member_perts, north, south, west, east, residual, lon, lat, increment
+    )
     return (increment, gradient)
 
 

time: 48.9 us -> 45 us (0.920)
  Pallas kernels: 47.1 us -> 43.9 us
  local copies, waits for them, and re-layouts: 0.8 us -> 0 us
    pallas_call x1, Pallas kernels: 34.2 us -> 31 us  [core_step(): pl.pallas_call(core_kernel, in_specs=[pl.BlockSpec(memory_space=pltpu.SME...]
    unnamed x3 -> x0, local copies, waits for them, and re-layouts: 0.8 us -> none
where the time goes in v1:
time: 45 us; the launch traced here: 44.6 us
  Pallas kernels  43.9 us (98%)
  between operations  0.64 us (1%)
    pallas_call x1, Pallas kernels, core_step(): pl.pallas_call(core_kernel, in_specs=[pl.BlockSpec(memory_space=pltpu.SME...  31 us
    pallas_call x1, Pallas kernels, adjoint(): pl.pallas_call(adjoint_kernel, grid=(members // GROUP, levels), in_specs=...  13 us

profile of v1, /device:TPU:0, one launch (start us, length us, event | category | flops | bytes accessed | tf_op | source)
XLA Modules:
  0.0 44.6 jit_solution(18283341065224924235)
XLA Ops:
  0.6 31.0 %shard_map.104 = (f32[2,256,256]{2,1,0:T(8,128)}, f32[2,144,256]{2,1,0:T(8,128)}, bf16[40,2,8,128]{3,2,1,0:T(8,128)(2,1)}, bf16[40,2,8,128]{3,2,1,0:T(8,128)(2,1...) custom-call(s32[2]{0:T(128)} %widths.1, ...), custom_call_target="tpu_custom_call" | custom-call | flops 1073741824 | bytes 16777216 | tf_op jit(solution)/shard_map/pallas_call | solution.py:616
  31.6 13.0 %shard_map.105 = (f32[40,2,128,128]{3,2,1,0:T(8,128)}, f32[2,256,256]{2,1,0:T(8,128)}) custom-call(bf16[40,2,128,128]{3,2,1,0:T(8,128)(2,1)} %alpha.3, bf16[40,2,128,128]{3,2,1,0:T(8,128)(2,1)} %perts.3, bf16[40,2,8,128]{3,2,1,0:T(8,128)(2,1)} %get-tuple-element.12.north, bf16[40,2,8,128]{3,2,1,0:T(8,128)(2,1)} %get-tuple-element.13.south, ...), custom_call_target="tpu_custom_call" | custom-call | flops 2684354560 | bytes 10485760 | tf_op jit(solution)/shard_map/pallas_call | solution.py:704

commit v2 on v1

--- a/solution.py
+++ b/solution.py
@@ -1,3 +1,5 @@
+import math
+
 import jax
 import jax.numpy as jnp
 from jax import lax
@@ -14,7 +16,9 @@
 STRIP = 24
 REACH = HB + 10
 MESH = pl.DeviceIdType.MESH
-VMEM_LIMIT = 60 * 2**20
+VMEM_BYTES = 67043328
+VMEM_SLACK = 2**17
+BACK_LIMIT = 32 * 2**20
 F32 = jnp.float32
 BF16 = jnp.bfloat16
 
@@ -160,13 +164,13 @@
                 )
 
     below, above = jnp.minimum(gy, 1), jnp.minimum(gyn - 1 - gy, 1)
-    pl.semaphore_wait(barrier, 2 + (count - 1) + (below + above) * (count + 2))
+    return lambda: pl.semaphore_wait(barrier, 2 + (count - 1) + (below + above) * (count + 2))
 
 
 def core_kernel(
     widths, lat_i, lat_w, lon_i, lon_w, alpha, perts, innov, weight,
-    increment, residual, p_north, p_south, p_west, p_east, lon_taps, lat_back,
-    a_tile, p_tile, fine_tile, pick, edge_taps, lat_fore, v_strip, v_side, p_right, p_left,
+    increment, residual, a_tile, p_tile, p_north, p_south, p_west, p_east, lon_taps, lat_back,
+    fine_tile, pick, edge_taps, lat_fore, v_strip, v_side, p_right, p_left,
     f_low, f_high, f_right, f_left, f_west, f_east, fine_wide,
     lat_i_low, lat_i_high, lat_w_low, lat_w_high, lon_i_west, lon_i_east, lon_w_west, lon_w_east,
     up_lon, up_lat, down_lat, down_lon, ext, other, low, high, to_east, to_west, from_west, from_east,
@@ -177,6 +181,7 @@
     frows, fcols = innov.shape[1:]
     ma, count = lax.axis_index("ma"), lax.axis_size("ma")
     gx, gxn = lax.axis_index("gx"), lax.axis_size("gx")
+    met = greet()
     f_loads = [
         pltpu.make_async_copy(src.at[ma], fine_tile.at[i], local.at[i])
         for i, src in enumerate((innov, weight))
@@ -187,7 +192,7 @@
         return pltpu.make_async_copy(src.at[span], dst.at[span], local.at[first + g])
 
     p_loads = [group_load(perts, p_tile, g, 2) for g in range(steps)]
-    for load in f_loads + p_loads:
+    for load in p_loads + f_loads:
         load.start()
     counter = iter(range(96))
     pending = []
@@ -208,8 +213,6 @@
             at = slice(k % 2 * cols, (k % 2 + 1) * cols)
             n = l * GROUP + k
             pick[n // 2, at] = jnp.where(slot == n, base, 0.0).astype(BF16)
-    greet()
-
     f_rows = [
         link("gy", 1, innov.at[ma, pl.ds(frows - FR, FR)], f_low.at[0]),
         link("gy", -1, innov.at[ma, pl.ds(0, FR)], f_high.at[0]),
@@ -230,9 +233,6 @@
         link("gx", 1, lon_w, lon_w_west),
         link("gx", -1, lon_w, lon_w_east),
     ]
-    for one in small + f_rows + p_rows:
-        one.start()
-
     def tilted(src, dst, side, top, bottom, first):
         pairs = []
         for step, at, to in ((1, bottom, first), (-1, top, first + HB)):
@@ -249,6 +249,41 @@
             )
         return pairs
 
+    def packed(piece):
+        total = None
+        for l in range(levels):
+            for k in range(0, GROUP, 2):
+                n = (l * GROUP + k) // 2
+                part = dot(lanes_of(piece(l, k), piece(l, k + 1)), pick[n])
+                total = part if total is None else total + part
+        return total.astype(BF16)
+
+    a_loads = [group_load(alpha, a_tile, g, 2 + steps) for g in range(steps)]
+    p_arrive = []
+    for g in range(steps):
+        p_loads[g].wait()
+        a_loads[g].start()
+        both = packed(lambda l, k: p_tile[g * GROUP + k, l])
+        p_right[g] = both[:, :cols]
+        p_left[g] = both[:, cols:]
+        if g == 0:
+            met()
+            for one in small + p_rows:
+                one.start()
+        span = pl.ds(0, rows)
+        pair = [
+            link("gx", 1, p_right.at[g], p_west.at[g, span]),
+            link("gx", -1, p_left.at[g], p_east.at[g, span]),
+        ]
+        for one in pair:
+            one.start()
+        p_arrive += pair
+    corners = tilted(p_right, p_west, 1, 0, rows - HB, rows)
+    corners += tilted(p_left, p_east, gxn - 1, 0, rows - HB, rows)
+    for one in corners + f_rows:
+        one.start()
+    p_arrive += corners
+
     f_main = f_west.shape[0] - 2 * HB
 
     def f_fold(first, count, start):
@@ -278,37 +313,6 @@
     for one in f_arrive:
         one.start()
 
-    def packed(piece):
-        total = None
-        for l in range(levels):
-            for k in range(0, GROUP, 2):
-                n = (l * GROUP + k) // 2
-                part = dot(lanes_of(piece(l, k), piece(l, k + 1)), pick[n])
-                total = part if total is None else total + part
-        return total.astype(BF16)
-
-    a_loads = [group_load(alpha, a_tile, g, 2 + steps) for g in range(steps)]
-    p_arrive = []
-    for g in range(steps):
-        p_loads[g].wait()
-        a_loads[g].start()
-        both = packed(lambda l, k: p_tile[g * GROUP + k, l])
-        p_right[g] = both[:, :cols]
-        p_left[g] = both[:, cols:]
-        span = pl.ds(0, rows)
-        pair = [
-            link("gx", 1, p_right.at[g], p_west.at[g, span]),
-            link("gx", -1, p_left.at[g], p_east.at[g, span]),
-        ]
-        for one in pair:
-            one.start()
-        p_arrive += pair
-    corners = tilted(p_right, p_west, 1, 0, rows - HB, rows)
-    corners += tilted(p_left, p_east, gxn - 1, 0, rows - HB, rows)
-    for one in corners:
-        one.start()
-    p_arrive += corners
-
     lane = iota((cols, cols), 1)
     deep = half + 2 * HB
     wide_k = lat_fore.shape[3]
@@ -317,7 +321,10 @@
         scale = tap_scale(spread)
         cell, at = iota((cols, cols), 0), lane
         lon_taps[l, 0], lon_taps[l, 1] = split(tap_value(cell - at, spread, scale))
-        lon_taps[l, 2], lon_taps[l, 3] = split(tap_value(side_cell(cell, l, cols) - at, spread, scale))
+        shift = at % (2 * HB)
+        gap = side_cell(cell, l, cols) - jnp.where(shift < HB, cols - HB + shift, shift - HB)
+        own = cell % slots // HB == at // (2 * HB)
+        lon_taps[l, 2], lon_taps[l, 3] = split(jnp.where(own, tap_value(gap, spread, scale), 0.0))
         edge_taps[l, 0], edge_taps[l, 1] = split(tap_value(side_cell(at, l, cols) - cell, spread, scale))
         lat_back[l] = lat_taps(spread, scale, half, deep, -HB, wide_k)
         lat_fore[l, 0] = lat_taps(spread, scale, deep, deep, HB, wide_k)
@@ -566,6 +573,8 @@
     outs = [
         (innov.shape, F32),
         ((levels, e_rows, 2 * cols), F32),
+        (alpha.shape, BF16),
+        (alpha.shape, BF16),
         strip,
         strip,
         side,
@@ -573,12 +582,11 @@
         ((levels, 4, cols, cols), BF16),
         ((levels, half, wide_k), BF16),
     ]
+    kept = sum(math.prod(shape) * jnp.dtype(kind).itemsize for shape, kind in outs)
     fine_edge = ((2, FR, fcols), F32)
     fine_side = ((-(-frows // (FOLD * HB)) * HB + 2 * HB, cols), F32)
     packed = ((steps, rows, cols), BF16)
     scratch = [
-        (alpha.shape, BF16),
-        (alpha.shape, BF16),
         ((2, frows, fcols), F32),
         ((levels * GROUP // 2, 2 * cols, 2 * cols), BF16),
         ((levels, 2, cols, cols), BF16),
@@ -612,12 +620,12 @@
         ((count, STRIP, 2 * cols), F32),
     ] + [((STRIP, cols), F32)] * 4
     vmem = pl.BlockSpec(memory_space=pltpu.VMEM)
-    anywhere = pl.BlockSpec(memory_space=pl.ANY)
+    anywhere = pl.BlockSpec(memory_space=pltpu.HBM)
     return pl.pallas_call(
         core_kernel,
         in_specs=[pl.BlockSpec(memory_space=pltpu.SMEM)] + [vmem] * 4 + [anywhere] * 4,
         out_specs=[vmem] * len(outs),
-        out_shape=[jax.ShapeDtypeStruct(shape, kind) for shape, kind in outs],
+        out_shape=[pltpu.VMEM(shape, kind) for shape, kind in outs],
         scratch_shapes=[pltpu.VMEM(shape, kind) for shape, kind in scratch]
         + [
             pltpu.SemaphoreType.DMA((96,)),
@@ -625,7 +633,7 @@
             pltpu.SemaphoreType.DMA((2 + 2 * steps,)),
         ],
         compiler_params=pltpu.CompilerParams(
-            collective_id=0, has_side_effects=True, vmem_limit_bytes=VMEM_LIMIT
+            collective_id=0, has_side_effects=True, vmem_limit_bytes=VMEM_BYTES - VMEM_SLACK - kept
         ),
         cost_estimate=cost(2**30, 2**24),
     )(widths, lat_i, lat_w, lon_i, lon_w, alpha, perts, innov, weight)
@@ -642,76 +650,73 @@
 
 
 def adjoint_kernel(
-    alpha, perts, north, south, west, east, residual, lon, lat, fine, out, fine_out, held, sems
+    alpha, perts, north, south, west, east, residual, lon, lat, fine, out, fine_out, sem
 ):
     rows, cols = alpha.shape[2:]
     slots = GROUP * HB
-    g, l = pl.program_id(0), pl.program_id(1)
-    take = pltpu.make_async_copy(fine, held, sems.at[0])
-    give = pltpu.make_async_copy(held, fine_out, sems.at[1])
-
-    @pl.when((g == 0) & (l == 0))
+    g = pl.program_id(0)
+    give = pltpu.make_async_copy(fine, fine_out, sem.at[0])
+
+    @pl.when(g == 0)
     def _():
-        take.start()
-
-    @pl.when((g == 1) & (l == 0))
-    def _():
-        take.wait()
         give.start()
 
-    @pl.when((g == pl.num_programs(0) - 1) & (l == pl.num_programs(1) - 1))
+    @pl.when(g == pl.num_programs(0) - 1)
     def _():
         give.wait()
 
-    res = residual[l]
-    wide = iota((rows + 2 * HB, cols), 1)
-    side = jnp.where(wide // slots == l, west[0].astype(F32), east[0].astype(F32))
-    side = natural(side, rows) * res[:, cols:]
-    taps = lat[l, :, : 3 * (rows // 2 + 2 * HB)]
     zero = jnp.zeros((cols, cols), BF16)
 
     def stack(high, low):
         return rows_of(lanes_of(high, low), lanes_of(high, zero))
 
-    core, wing = stack(lon[l, 0], lon[l, 1]), stack(lon[l, 2], lon[l, 3])
-    edge_h, edge_l = split(band(*split(side), taps))
+    def halves(x):
+        return x[:, :cols] + x[:, cols:]
+
     lane = iota((rows, cols), 1)
-    for k in range(0, GROUP, 2):
-        pairs = []
-        for m in (k, k + 1):
-            tall = rows_of(north[m, 0].astype(F32), perts[m, 0].astype(F32), south[m, 0].astype(F32))
-            pairs.append(split(tall * res[:, :cols]))
-        both = band(lanes_of(pairs[0][0], pairs[1][0]), lanes_of(pairs[0][1], pairs[1][1]), taps)
-        for i, m in enumerate((k, k + 1)):
-            mine = lane % slots // HB == m
-            edges = lanes_of(
-                jnp.where(mine, edge_h, jnp.zeros_like(edge_h)),
-                jnp.where(mine, edge_l, jnp.zeros_like(edge_l)),
-            )
-            total = dot(lanes_of(*split(both[:, i * cols : (i + 1) * cols])), core) + dot(edges, wing)
-            out[m, 0] = alpha[m, 0].astype(F32) + (total[:, :cols] + total[:, cols:])
+    inner = (lane >= HB) & (lane < cols - HB)
+    wide = iota((rows + 2 * HB, cols), 1)
+    for l in range(alpha.shape[1]):
+        res = residual[l]
+        taps = lat[l, :, : 3 * (rows // 2 + 2 * HB)]
+        side = jnp.where(wide // slots == l, west[g].astype(F32), east[g].astype(F32))
+        edge = band(*split(natural(side, rows) * res[:, cols:]), taps)
+        edge = halves(dot(lanes_of(*split(edge)), stack(lon[l, 2], lon[l, 3])))
+        cores = []
+        for k in range(0, GROUP, 2):
+            pairs = []
+            for m in (k, k + 1):
+                n = g * GROUP + m
+                tall = rows_of(
+                    north[n, l].astype(F32), perts[n, l].astype(F32), south[n, l].astype(F32)
+                )
+                pairs.append(split(tall * res[:, :cols]))
+            both = band(lanes_of(pairs[0][0], pairs[1][0]), lanes_of(pairs[0][1], pairs[1][1]), taps)
+            for i in range(2):
+                cores.append(lanes_of(*split(both[:, i * cols : (i + 1) * cols])))
+        total = dot(rows_of(*cores), stack(lon[l, 0], lon[l, 1]))
+        for m in range(GROUP):
+            turned = pltpu.roll(edge, (cols - HB - 2 * HB * m) % cols, 1)
+            value = halves(total[m * rows : (m + 1) * rows]) + jnp.where(inner, 0.0, turned)
+            out[m, l] = alpha[g * GROUP + m, l].astype(F32) + value
 
 
 def adjoint(alpha, perts, north, south, west, east, residual, lon, lat, fine):
     members, levels, rows, cols = alpha.shape
-    block = pl.BlockSpec((GROUP, 1, rows, cols), lambda g, l: (g, l, 0, 0))
-    strip = pl.BlockSpec((GROUP, 1, HB, cols), lambda g, l: (g, l, 0, 0))
-    side = pl.BlockSpec((1, rows + 2 * HB, cols), lambda g, l: (g, 0, 0))
-
-    def whole(x):
-        return pl.BlockSpec(x.shape, lambda g, l: (0,) * x.ndim)
-
     return pl.pallas_call(
         adjoint_kernel,
-        grid=(members // GROUP, levels),
-        in_specs=[block, block, strip, strip, side, side, whole(residual), whole(lon), whole(lat)]
-        + [pl.BlockSpec(memory_space=pl.ANY)],
-        out_specs=[block, pl.BlockSpec(memory_space=pl.ANY)],
+        grid=(members // GROUP,),
+        in_specs=[pl.BlockSpec(memory_space=pltpu.VMEM)] * 10,
+        out_specs=[
+            pl.BlockSpec((GROUP, levels, rows, cols), lambda g: (g, 0, 0, 0)),
+            pl.BlockSpec(memory_space=pltpu.HBM),
+        ],
         out_shape=[
             jax.ShapeDtypeStruct(alpha.shape, F32),
             jax.ShapeDtypeStruct(fine.shape, F32),
         ],
-        scratch_shapes=[pltpu.VMEM(fine.shape, F32), pltpu.SemaphoreType.DMA((2,))],
+        scratch_shapes=[pltpu.SemaphoreType.DMA((1,))],
+        compiler_params=pltpu.CompilerParams(vmem_limit_bytes=BACK_LIMIT),
         cost_estimate=cost(members * levels * 2**25, alpha.size * 8),
     )(alpha, perts, north, south, west, east, residual, lon, lat, fine)
 
@@ -728,12 +733,12 @@
     obs_weight,
 ):
     tables = [x.reshape(1, -1) for x in (lat_index, lat_weight, lon_index, lon_weight)]
-    increment, residual, *halos = core_step(
+    increment, residual, alpha, perts, *rest = core_step(
         band_widths, *tables, alpha_fields, member_perts, innovation, obs_weight
     )
-    north, south, west, east, lon, lat = halos
+    north, south, west, east, lon, lat = rest
     gradient, increment = adjoint(
-        alpha_fields, member_perts, north, south, west, east, residual, lon, lat, increment
+        alpha, perts, north, south, west, east, residual, lon, lat, increment
     )
     return (increment, gradient)
 

time: 45 us -> 36.6 us (0.81)
  Pallas kernels: 43.9 us -> 35.8 us
    pallas_call x1, Pallas kernels: 13 us -> 6.2 us  [adjoint(): pl.pallas_call(adjoint_kernel, grid=(members // GROUP,), in_specs=[pl.Blo...]
    pallas_call x1, Pallas kernels: 31 us -> 29.6 us  [core_step(): pl.pallas_call(core_kernel, in_specs=[pl.BlockSpec(memory_space=pltpu.SME...]
where the time goes in v2:
time: 36.6 us; the launch traced here: 36.4 us
  Pallas kernels  35.8 us (98%)
  between operations  0.64 us (2%)
    pallas_call x1, Pallas kernels, core_step(): pl.pallas_call(core_kernel, in_specs=[pl.BlockSpec(memory_space=pltpu.SME...  29.6 us
    pallas_call x1, Pallas kernels, adjoint(): pl.pallas_call(adjoint_kernel, grid=(members // GROUP,), in_specs=[pl.Blo...  6.2 us

profile of v2, /device:TPU:0, one launch (start us, length us, event | category | flops | bytes accessed | tf_op | source)
XLA Modules:
  0.0 36.4 jit_solution(16771157947818081638)
XLA Ops:
  0.6 29.6 %shard_map.104 = (f32[2,256,256]{2,1,0:T(8,128)S(1)}, f32[2,144,256]{2,1,0:T(8,128)S(1)}, bf16[40,2,128,128]{3,2,1,0:T(8,128)(2,1)S(1)}, bf16[40,2,128,128]{3,2,...) custom-call(s32[2]{0:T(128)} %widths.1, ...), custom_call_target="tpu_custom_call" | custom-call | flops 1073741824 | bytes 16777216 | tf_op jit(solution)/shard_map/pallas_call | solution.py:624
  30.2 6.2 %shard_map.105 = (f32[40,2,128,128]{3,2,1,0:T(8,128)}, f32[2,256,256]{2,1,0:T(8,128)}) custom-call(bf16[40,2,128,128]{3,2,1,0:T(8,128)(2,1)S(1)} %get-tuple-element.14.alpha, bf16[40,2,128,128]{3,2,1,0:T(8,128)(2,1)S(1)} %get-tuple-element.15.perts, bf16[40,2,8,128]{3,2,1,0:T(8,128)(2,1)S(1)} %get-tuple-element.16.north, ...), custom_call_target="tpu_custom_call" | custom-call | flops 2684354560 | bytes 10485760 | tf_op jit(solution)/shard_map/pallas_call | solution.py:706

commit v3 on v2

--- a/solution.py
+++ b/solution.py
@@ -136,35 +136,26 @@
     gx, gxn = lax.axis_index("gx"), lax.axis_size("gx")
     gy, gyn = lax.axis_index("gy"), lax.axis_size("gy")
     ma, count = lax.axis_index("ma"), lax.axis_size("ma")
-    for step in (1, gxn - 1):
-        pl.semaphore_signal(
-            barrier, inc=1, device_id={"gx": lax.rem(gx + step, gxn)}, device_id_type=MESH
-        )
-    for s in range(1, count):
-        pl.semaphore_signal(
-            barrier, inc=1, device_id={"ma": lax.rem(ma + s, count)}, device_id_type=MESH
-        )
-    for step, there in ((-1, gy > 0), (1, gy < gyn - 1)):
-
-        @pl.when(there)
-        def _(step=step):
-            for s in range(count):
-                pl.semaphore_signal(
-                    barrier,
-                    inc=1,
-                    device_id={"gy": gy + step, "ma": lax.rem(ma + s, count)},
-                    device_id_type=MESH,
-                )
-            for side in (1, gxn - 1):
-                pl.semaphore_signal(
-                    barrier,
-                    inc=1,
-                    device_id={"gx": lax.rem(gx + side, gxn), "gy": gy + step},
-                    device_id_type=MESH,
-                )
+
+    def hail(device):
+        pl.semaphore_signal(barrier, inc=1, device_id=device, device_id_type=MESH)
+
+    for s in range(count):
+        peer = lax.rem(ma + s, count)
+        if s:
+            hail({"ma": peer})
+        sides = [lax.rem(gx + step, gxn) for step in (1, gxn - 1)]
+        for side in sides:
+            hail({"gx": side, "ma": peer})
+        for step, there in ((-1, gy > 0), (1, gy < gyn - 1)):
+
+            @pl.when(there)
+            def _(step=step, peer=peer, sides=sides):
+                for side in (gx, *sides):
+                    hail({"gx": side, "gy": gy + step, "ma": peer})
 
     below, above = jnp.minimum(gy, 1), jnp.minimum(gyn - 1 - gy, 1)
-    return lambda: pl.semaphore_wait(barrier, 2 + (count - 1) + (below + above) * (count + 2))
+    return lambda: pl.semaphore_wait(barrier, 3 * count - 1 + (below + above) * 3 * count)
 
 
 def core_kernel(
@@ -173,7 +164,7 @@
     fine_tile, pick, edge_taps, lat_fore, v_strip, v_side, p_right, p_left,
     f_low, f_high, f_right, f_left, f_west, f_east, fine_wide,
     lat_i_low, lat_i_high, lat_w_low, lat_w_high, lon_i_west, lon_i_east, lon_w_west, lon_w_east,
-    up_lon, up_lat, down_lat, down_lon, ext, other, low, high, to_east, to_west, from_west, from_east,
+    up_lon, up_lat, down_lat, down_lon, ext, other, ends_in, flank, tip, flanks, tips,
     send, recv, local,
 ):
     members, levels, rows, cols = alpha.shape
@@ -260,6 +251,16 @@
 
     a_loads = [group_load(alpha, a_tile, g, 2 + steps) for g in range(steps)]
     p_arrive = []
+    def p_sides(g):
+        span = pl.ds(0, rows)
+        pair = [
+            link("gx", 1, p_right.at[g], p_west.at[g, span]),
+            link("gx", -1, p_left.at[g], p_east.at[g, span]),
+        ]
+        for one in pair:
+            one.start()
+        p_arrive.append(pair)
+
     for g in range(steps):
         p_loads[g].wait()
         a_loads[g].start()
@@ -270,19 +271,15 @@
             met()
             for one in small + p_rows:
                 one.start()
-        span = pl.ds(0, rows)
-        pair = [
-            link("gx", 1, p_right.at[g], p_west.at[g, span]),
-            link("gx", -1, p_left.at[g], p_east.at[g, span]),
-        ]
-        for one in pair:
-            one.start()
-        p_arrive += pair
+            p_sides(g)
     corners = tilted(p_right, p_west, 1, 0, rows - HB, rows)
     corners += tilted(p_left, p_east, gxn - 1, 0, rows - HB, rows)
-    for one in corners + f_rows:
+    for one in corners:
         one.start()
-    p_arrive += corners
+    for g in range(1, steps):
+        p_sides(g)
+    for one in f_rows:
+        one.start()
 
     f_main = f_west.shape[0] - 2 * HB
 
@@ -349,16 +346,16 @@
             taps = rows_of(
                 lanes_of(lon_taps[l, 0], edge_taps[l, 0]), lanes_of(lon_taps[l, 1], edge_taps[l, 1])
             )
-            side = total = None
+            fields = [a_tile[g * GROUP + m, l] for m in range(GROUP)]
+            u = dot(rows_of(*[lanes_of(a, a) for a in fields]), taps)
+            side = u[:rows, cols:]
+            for m in range(1, GROUP):
+                mine = lane % slots // HB == m
+                side = jnp.where(mine, u[m * rows : (m + 1) * rows, cols:], side)
+            total = None
             for k in range(0, GROUP, 2):
-                cores = []
-                for m in (k, k + 1):
-                    a = a_tile[g * GROUP + m, l]
-                    u = dot(lanes_of(a, a), taps)
-                    cores.append(u[:, :cols])
-                    mine = lane % slots // HB == m
-                    side = u[:, cols:] if side is None else jnp.where(mine, u[:, cols:], side)
-                top, bottom = tall(lanes_of(*cores), l)
+                pair = [u[m * rows : (m + 1) * rows, :cols] for m in (k, k + 1)]
+                top, bottom = tall(lanes_of(*pair), l)
                 for i, m in enumerate((k, k + 1)):
                     at = slice(i * cols, (i + 1) * cols)
                     v = rows_of(top[HB:, at], bottom[:half, at])
@@ -454,100 +451,118 @@
             rows_of(fine_tile[i], f_low[i], f_high[i]), wing_of(f_west), wing_of(f_east)
         )
 
-    for one in p_arrive:
+    thick = iota((rows, cols), 1) // slots
+    thin = iota((2 * HB, cols), 1) // slots
+    side_sums = [None] * levels
+    for g in range(steps):
+        for one in p_arrive[g]:
+            one.arrive()
+        for l in range(levels):
+            west, east = p_west[g, :rows].astype(F32), p_east[g, :rows].astype(F32)
+            part = jnp.where(thick == l, west, east) * v_side[g, l, HB : HB + rows]
+            side_sums[l] = part if g == 0 else side_sums[l] + part
+    for one in corners:
         one.arrive()
-    tall_lane = iota((e_rows, cols), 1)
+    t_lane, e_lane = iota((t_rows, cols), 1), iota((e_rows, cols), 1)
+
+    def fold(x, first, deep):
+        total = None
+        lane_at = iota((deep, cols), 1)
+        for b in range(x.shape[0] // deep):
+            part = pltpu.roll(x[b * deep : (b + 1) * deep], (b * REACH - first) % cols, 1)
+            total = part if total is None else jnp.where(lane_at >= b * REACH, part, total)
+        return total
+
+    def unfold(x, first, start, blocks):
+        parts = [pltpu.roll(x, (first - b * REACH) % cols, 1) for b in range(start, start + blocks)]
+        return rows_of(*parts)
+
     for l in range(levels):
-        total = None
+        ends = None
         for g in range(steps):
-            side = jnp.where(
-                tall_lane // slots == l, p_west[g].astype(F32), p_east[g].astype(F32)
-            )
-            part = natural(side, rows) * v_side[g, l]
-            total = part if total is None else total + part
-        ext[l, :, cols:] = total if l == 0 else pltpu.roll(total, slots, 1)
-
-    swaps, lows, highs = [], [], []
+            west, east = p_west[g, rows:].astype(F32), p_east[g, rows:].astype(F32)
+            v = rows_of(v_side[g, l, :HB], v_side[g, l, HB + rows :])
+            part = jnp.where(thin == l, west, east) * v
+            ends = part if ends is None else ends + part
+        side = rows_of(ends[:HB], side_sums[l], ends[HB:])
+        if l:
+            side = pltpu.roll(side, slots, 1)
+        for shift in (HB, 2 * HB, 4 * HB):
+            side = side + pltpu.roll(side, shift, 1)
+        ext[l, :, cols:] = side
+        core = ext[l, :, :cols]
+        eastward = jnp.where(e_lane >= cols - HB, side, pltpu.roll(core, cols - HB, 1))
+        westward = jnp.where(e_lane < slots, side, pltpu.roll(core, slots, 1))
+        for i, (x, first) in enumerate(((eastward, cols - REACH), (westward, slots - HB))):
+            flank[l, i] = fold(x, first, STRIP)
+            tip[l, i] = fold(rows_of(x[e_rows - STRIP :], x[:STRIP]), first, HB)
+
+    sent = []
     for s in range(count):
         peer = lax.rem(ma + s, count)
+        for i, step in enumerate((1, -1)):
+            side = lax.rem(gx + step + gxn, gxn)
+            sent.append(link("gx", step, flank.at[peer, i], flanks.at[s, i], {"ma": peer}))
+            for j, turn in enumerate((1, -1)):
+                at = {"gx": side, "ma": peer}
+                sent.append(link("gy", turn, tip.at[peer, i], tips.at[s, i, j], at))
+        sent.append(link("gy", 1, ext.at[peer, pl.ds(e_rows - STRIP, STRIP)], ends_in.at[s, 0], {"ma": peer}))
+        sent.append(link("gy", -1, ext.at[peer, pl.ds(0, STRIP)], ends_in.at[s, 1], {"ma": peer}))
         if s:
-            swaps.append(link("ma", peer - ma, ext.at[peer], other.at[s - 1]))
-        lows.append(link("gy", 1, ext.at[peer, pl.ds(e_rows - STRIP, STRIP)], low.at[s], {"ma": peer}))
-        highs.append(link("gy", -1, ext.at[peer, pl.ds(0, STRIP)], high.at[s], {"ma": peer}))
-    for one in lows + highs + swaps:
+            sent.append(link("ma", peer - ma, ext.at[peer], other.at[s - 1]))
+    for one in sent:
         one.start()
-    for one in swaps + lows + highs:
+    for one in sent:
         one.arrive()
-    mine = ext[ma]
-    for s in range(count - 1):
-        mine = mine + other[s]
-    above, below = low[0], high[0]
+    mine, strips_in, flank_in, tip_in = ext[ma], ends_in[0], flanks[0], tips[0]
     for s in range(1, count):
-        above, below = above + low[s], below + high[s]
+        mine = mine + other[s - 1]
+        strips_in, flank_in, tip_in = strips_in + ends_in[s], flank_in + flanks[s], tip_in + tips[s]
     lap = CR - HB
     edge = STRIP - lap
-    mine = rows_of(
-        above[:lap],
-        mine[:edge] + above[lap:],
-        mine[edge : e_rows - edge],
-        mine[e_rows - edge :] + below[:edge],
-        below[edge:],
-    )
+
+    def merge(above, middle, below):
+        return rows_of(
+            above[:lap],
+            middle[:edge] + above[lap:],
+            middle[edge : e_rows - edge],
+            middle[e_rows - edge :] + below[:edge],
+            below[edge:],
+        )
+
+    mine = merge(strips_in[0], mine, strips_in[1])
     core, side = mine[:, :cols], mine[:, cols:]
-    for shift in (HB, 2 * HB, 4 * HB):
-        side = side + pltpu.roll(side, shift, 1)
-
-    blocks = (t_rows + STRIP - 1) // STRIP
-    t_lane = iota((t_rows, cols), 1)
-    thin = iota((STRIP, cols), 1)
-
-    def fold(x, first):
-        if blocks * STRIP > t_rows:
-            x = rows_of(x, jnp.zeros((blocks * STRIP - t_rows, cols), F32))
-        total = None
-        for b in range(blocks):
-            part = pltpu.roll(x[b * STRIP : (b + 1) * STRIP], (b * REACH - first) % cols, 1)
-            total = part if total is None else jnp.where(thin >= b * REACH, part, total)
-        return total
-
-    def unfold(x, first):
-        parts = [pltpu.roll(x, (first - b * REACH) % cols, 1) for b in range(blocks)]
-        return rows_of(*parts)[:t_rows]
-
-    eastward = jnp.where(t_lane >= cols - HB, side, pltpu.roll(core, cols - HB, 1))
-    westward = jnp.where(t_lane < slots, side, pltpu.roll(core, slots, 1))
-    to_east[...] = fold(eastward, cols - REACH)
-    to_west[...] = fold(westward, slots - HB)
-    sides = [
-        link("gx", 1, to_east, from_west),
-        link("gx", -1, to_west, from_east),
-    ]
-    for one in sides:
-        one.start()
-    for one in sides:
-        one.arrive()
+    third = STRIP // HB
+
+    def wing_from(i, first):
+        return merge(
+            unfold(tip_in[i, 0], first, 0, third),
+            unfold(flank_in[i], first, 0, e_rows // STRIP),
+            unfold(tip_in[i, 1], first, third, third),
+        )
+
     wings = jnp.where(
         t_lane < REACH,
-        unfold(from_west[...], 0),
-        jnp.where((t_lane >= slots) & (t_lane < slots + REACH), unfold(from_east[...], slots), side),
+        wing_from(0, 0),
+        jnp.where((t_lane >= slots) & (t_lane < slots + REACH), wing_from(1, slots), side),
     )
     across = dot3(split(lanes_of(core, wings)), (up_lon[0], up_lon[1]))
     fine = dot3((up_lat[0], up_lat[1]), split(across))
     increment[ma] = fine[:frows, :fcols]
-    ends = []
+    final = []
 
     def share(whole):
         for s in range(1, count):
             peer = lax.rem(ma + s, count)
-            ends.append(link("ma", peer - ma, whole.at[ma], whole.at[ma]))
-            ends[-1].start()
+            final.append(link("ma", peer - ma, whole.at[ma], whole.at[ma]))
+            final[-1].start()
 
     share(increment)
     misfit = fine_wide[1] * (fine - fine_wide[0])
     across = dot3((down_lat[0], down_lat[1]), split(misfit))
     residual[ma] = dot3(split(across), (down_lon[0], down_lon[1]))
     share(residual)
-    for one in ends:
+    for one in final:
         one.arrive()
     for one in pending:
         one.sent()
@@ -563,6 +578,7 @@
     frows, fcols = innov.shape[1:]
     count = lax.axis_size("ma")
     assert levels == 2 and count == levels
+    assert (rows + 2 * HB) % STRIP == 0
     half = rows // 2
     deep = half + 2 * HB
     wide_k = -(-3 * deep // 128) * 128
@@ -616,9 +632,12 @@
         ((2, f_wide, 2 * cols), BF16),
         ((levels, e_rows, 2 * cols), F32),
         ((count - 1, e_rows, 2 * cols), F32),
-        ((count, STRIP, 2 * cols), F32),
-        ((count, STRIP, 2 * cols), F32),
-    ] + [((STRIP, cols), F32)] * 4
+        ((count, 2, STRIP, 2 * cols), F32),
+        ((levels, 2, STRIP, cols), F32),
+        ((levels, 2, HB, cols), F32),
+        ((count, 2, STRIP, cols), F32),
+        ((count, 2, 2, HB, cols), F32),
+    ]
     vmem = pl.BlockSpec(memory_space=pltpu.VMEM)
     anywhere = pl.BlockSpec(memory_space=pltpu.HBM)
     return pl.pallas_call(

time: 36.6 us -> 35.2 us (0.962)
  Pallas kernels: 35.8 us -> 34.4 us
    pallas_call x1, Pallas kernels: 29.6 us -> 28.2 us  [core_step(): pl.pallas_call(core_kernel, in_specs=[pl.BlockSpec(memory_space=pltpu.SME...]
where the time goes in v3:
time: 35.2 us; the launch traced here: 35 us
  Pallas kernels  34.4 us (98%)
  between operations  0.64 us (2%)
    pallas_call x1, Pallas kernels, core_step(): pl.pallas_call(core_kernel, in_specs=[pl.BlockSpec(memory_space=pltpu.SME...  28.2 us
    pallas_call x1, Pallas kernels, adjoint(): pl.pallas_call(adjoint_kernel, grid=(members // GROUP,), in_specs=[pl.Blo...  6.2 us

profile of v3, /device:TPU:0, one launch (start us, length us, event | category | flops | bytes accessed | tf_op | source)
XLA Modules:
  0.0 35.0 jit_solution(17748509612563504943)
XLA Ops:
  0.6 28.2 %shard_map.104 = (f32[2,256,256]{2,1,0:T(8,128)S(1)}, f32[2,144,256]{2,1,0:T(8,128)S(1)}, bf16[40,2,128,128]{3,2,1,0:T(8,128)(2,1)S(1)}, bf16[40,2,128,128]{3,2,...) custom-call(s32[2]{0:T(128)} %widths.1, ...), custom_call_target="tpu_custom_call" | custom-call | flops 1073741824 | bytes 16777216 | tf_op jit(solution)/shard_map/pallas_call | solution.py:643
  28.8 6.2 %shard_map.105 = (f32[40,2,128,128]{3,2,1,0:T(8,128)}, f32[2,256,256]{2,1,0:T(8,128)}) custom-call(bf16[40,2,128,128]{3,2,1,0:T(8,128)(2,1)S(1)} %get-tuple-element.14.alpha, bf16[40,2,128,128]{3,2,1,0:T(8,128)(2,1)S(1)} %get-tuple-element.15.perts, bf16[40,2,8,128]{3,2,1,0:T(8,128)(2,1)S(1)} %get-tuple-element.16.north, ...), custom_call_target="tpu_custom_call" | custom-call | flops 2684354560 | bytes 10485760 | tf_op jit(solution)/shard_map/pallas_call | solution.py:725

commit v4 on v3

--- a/solution.py
+++ b/solution.py
@@ -307,8 +307,6 @@
         span = pl.ds(0, f_main)
         f_arrive.append(link("gx", step, src.at[span], dst.at[span]))
         f_arrive += tilted(src, dst, side, f_main, f_main + HB, f_main)
-    for one in f_arrive:
-        one.start()
 
     lane = iota((cols, cols), 1)
     deep = half + 2 * HB
@@ -433,23 +431,8 @@
         ext[l, :HB, :cols] = north
         ext[l, HB + rows :, :cols] = south
 
-    for one in f_arrive:
-        one.arrive()
     for i in range(2):
-
-        def wing_of(part):
-            def opened(first, last):
-                lanes = range(FC * i, 2 * FOLD * FC, 2 * FC)
-                return [part[first:last, x : x + FC] for x in lanes]
-
-            low, high = f_main, f_main + HB
-            return rows_of(
-                rows_of(*opened(0, low))[:frows], *opened(low, high), *opened(high, high + HB)
-            )
-
-        fine_wide[i] = lanes_of(
-            rows_of(fine_tile[i], f_low[i], f_high[i]), wing_of(f_west), wing_of(f_east)
-        )
+        fine_wide[i, :, :fcols] = rows_of(fine_tile[i], f_low[i], f_high[i])
 
     thick = iota((rows, cols), 1) // slots
     thin = iota((2 * HB, cols), 1) // slots
@@ -497,20 +480,21 @@
             flank[l, i] = fold(x, first, STRIP)
             tip[l, i] = fold(rows_of(x[e_rows - STRIP :], x[:STRIP]), first, HB)
 
-    sent = []
+    corner_links, side_links, end_links, swaps = [], [], [], []
     for s in range(count):
         peer = lax.rem(ma + s, count)
         for i, step in enumerate((1, -1)):
-            side = lax.rem(gx + step + gxn, gxn)
-            sent.append(link("gx", step, flank.at[peer, i], flanks.at[s, i], {"ma": peer}))
+            at = {"ma": peer}
+            side_links.append(link("gx", step, flank.at[peer, i], flanks.at[s, i], at))
+            strip = ext.at[peer, pl.ds((e_rows - STRIP) * (1 - i), STRIP)]
+            end_links.append(link("gy", step, strip, ends_in.at[s, i], at))
+            at = {"gx": lax.rem(gx + step + gxn, gxn), "ma": peer}
             for j, turn in enumerate((1, -1)):
-                at = {"gx": side, "ma": peer}
-                sent.append(link("gy", turn, tip.at[peer, i], tips.at[s, i, j], at))
-        sent.append(link("gy", 1, ext.at[peer, pl.ds(e_rows - STRIP, STRIP)], ends_in.at[s, 0], {"ma": peer}))
-        sent.append(link("gy", -1, ext.at[peer, pl.ds(0, STRIP)], ends_in.at[s, 1], {"ma": peer}))
+                corner_links.append(link("gy", turn, tip.at[peer, i], tips.at[s, i, j], at))
         if s:
-            sent.append(link("ma", peer - ma, ext.at[peer], other.at[s - 1]))
-    for one in sent:
+            swaps.append(link("ma", peer - ma, ext.at[peer], other.at[s - 1]))
+    sent = corner_links + side_links + end_links + swaps
+    for one in sent + f_arrive:
         one.start()
     for one in sent:
         one.arrive()
@@ -558,6 +542,21 @@
             final[-1].start()
 
     share(increment)
+    for one in f_arrive:
+        one.arrive()
+    for i in range(2):
+
+        def wing_of(part):
+            def opened(first, last):
+                lanes = range(FC * i, 2 * FOLD * FC, 2 * FC)
+                return [part[first:last, x : x + FC] for x in lanes]
+
+            low, high = f_main, f_main + HB
+            return rows_of(
+                rows_of(*opened(0, low))[:frows], *opened(low, high), *opened(high, high + HB)
+            )
+
+        fine_wide[i, :, fcols:] = lanes_of(wing_of(f_west), wing_of(f_east))
     misfit = fine_wide[1] * (fine - fine_wide[0])
     across = dot3((down_lat[0], down_lat[1]), split(misfit))
     residual[ma] = dot3(split(across), (down_lon[0], down_lon[1]))
@@ -669,21 +668,23 @@
 
 
 def adjoint_kernel(
-    alpha, perts, north, south, west, east, residual, lon, lat, fine, out, fine_out, sem
+    alpha, perts, north, south, west, east, residual, lon, lat, fine, out, fine_out, held, sem, fine_sem
 ):
-    rows, cols = alpha.shape[2:]
+    levels, rows, cols = alpha.shape[1:]
     slots = GROUP * HB
-    g = pl.program_id(0)
-    give = pltpu.make_async_copy(fine, fine_out, sem.at[0])
+    g, steps = pl.program_id(0), pl.num_programs(0)
+    give = pltpu.make_async_copy(fine, fine_out, fine_sem)
+    slot = lax.rem(g, 2)
+
+    def store(step, l):
+        at = lax.rem(step, 2)
+        target = out.at[pl.ds(step * GROUP, GROUP), l]
+        return pltpu.make_async_copy(held.at[at, l], target, sem.at[at, l])
 
     @pl.when(g == 0)
     def _():
         give.start()
 
-    @pl.when(g == pl.num_programs(0) - 1)
-    def _():
-        give.wait()
-
     zero = jnp.zeros((cols, cols), BF16)
 
     def stack(high, low):
@@ -695,7 +696,12 @@
     lane = iota((rows, cols), 1)
     inner = (lane >= HB) & (lane < cols - HB)
     wide = iota((rows + 2 * HB, cols), 1)
-    for l in range(alpha.shape[1]):
+    for l in range(levels):
+
+        @pl.when(g >= 2)
+        def _(l=l):
+            store(g - 2, l).wait()
+
         res = residual[l]
         taps = lat[l, :, : 3 * (rows // 2 + 2 * HB)]
         side = jnp.where(wide // slots == l, west[g].astype(F32), east[g].astype(F32))
@@ -717,7 +723,16 @@
         for m in range(GROUP):
             turned = pltpu.roll(edge, (cols - HB - 2 * HB * m) % cols, 1)
             value = halves(total[m * rows : (m + 1) * rows]) + jnp.where(inner, 0.0, turned)
-            out[m, l] = alpha[g * GROUP + m, l].astype(F32) + value
+            held[slot, l, m] = alpha[g * GROUP + m, l].astype(F32) + value
+        store(g, l).start()
+
+    @pl.when(g == steps - 1)
+    def _():
+        give.wait()
+        for l in range(levels):
+            store(g - 1, l).wait()
+        for l in range(levels):
+            store(g, l).wait()
 
 
 def adjoint(alpha, perts, north, south, west, east, residual, lon, lat, fine):
@@ -726,15 +741,16 @@
         adjoint_kernel,
         grid=(members // GROUP,),
         in_specs=[pl.BlockSpec(memory_space=pltpu.VMEM)] * 10,
-        out_specs=[
-            pl.BlockSpec((GROUP, levels, rows, cols), lambda g: (g, 0, 0, 0)),
-            pl.BlockSpec(memory_space=pltpu.HBM),
-        ],
+        out_specs=[pl.BlockSpec(memory_space=pltpu.HBM)] * 2,
         out_shape=[
             jax.ShapeDtypeStruct(alpha.shape, F32),
             jax.ShapeDtypeStruct(fine.shape, F32),
         ],
-        scratch_shapes=[pltpu.SemaphoreType.DMA((1,))],
+        scratch_shapes=[
+            pltpu.VMEM((2, levels, GROUP, rows, cols), F32),
+            pltpu.SemaphoreType.DMA((2, levels)),
+            pltpu.SemaphoreType.DMA,
+        ],
         compiler_params=pltpu.CompilerParams(vmem_limit_bytes=BACK_LIMIT),
         cost_estimate=cost(members * levels * 2**25, alpha.size * 8),
     )(alpha, perts, north, south, west, east, residual, lon, lat, fine)

time: 35.2 us -> 35 us (level)
    pallas_call x1, Pallas kernels: 28.2 us -> 25.8 us  [core_step(): pl.pallas_call(core_kernel, in_specs=[pl.BlockSpec(memory_space=pltpu.SME...]
    pallas_call x1, Pallas kernels: 6.2 us -> 8.34 us  [adjoint(): pl.pallas_call(adjoint_kernel, grid=(members // GROUP,), in_specs=[pl.Blo...]
where the time goes in v4:
time: 35 us; the launch traced here: 34.8 us
  Pallas kernels  34.2 us (98%)
  between operations  0.64 us (2%)
    pallas_call x1, Pallas kernels, core_step(): pl.pallas_call(core_kernel, in_specs=[pl.BlockSpec(memory_space=pltpu.SME...  25.8 us
    pallas_call x1, Pallas kernels, adjoint(): pl.pallas_call(adjoint_kernel, grid=(members // GROUP,), in_specs=[pl.Blo...  8.34 us

profile of v4, /device:TPU:0, one launch (start us, length us, event | category | flops | bytes accessed | tf_op | source)
XLA Modules:
  0.0 34.8 jit_solution(5385624812591845341)
XLA Ops:
  0.6 25.8 %shard_map.104 = (f32[2,256,256]{2,1,0:T(8,128)S(1)}, f32[2,144,256]{2,1,0:T(8,128)S(1)}, bf16[40,2,128,128]{3,2,1,0:T(8,128)(2,1)S(1)}, bf16[40,2,128,128]{3,2,...) custom-call(s32[2]{0:T(128)} %widths.1, ...), custom_call_target="tpu_custom_call" | custom-call | flops 1073741824 | bytes 16777216 | tf_op jit(solution)/shard_map/pallas_call | solution.py:642
  26.5 8.3 %shard_map.105 = (f32[40,2,128,128]{3,2,1,0:T(8,128)}, f32[2,256,256]{2,1,0:T(8,128)}) custom-call(bf16[40,2,128,128]{3,2,1,0:T(8,128)(2,1)S(1)} %get-tuple-element.14.alpha, bf16[40,2,128,128]{3,2,1,0:T(8,128)(2,1)S(1)} %get-tuple-element.15.perts, bf16[40,2,8,128]{3,2,1,0:T(8,128)(2,1)S(1)} %get-tuple-element.16.north, ...), custom_call_target="tpu_custom_call" | custom-call | flops 2684354560 | bytes 10485760 | tf_op jit(solution)/shard_map/pallas_call | solution.py:740

commit v5 on v4

--- a/solution.py
+++ b/solution.py
@@ -668,23 +668,21 @@
 
 
 def adjoint_kernel(
-    alpha, perts, north, south, west, east, residual, lon, lat, fine, out, fine_out, held, sem, fine_sem
+    alpha, perts, north, south, west, east, residual, lon, lat, fine, out, fine_out, sem
 ):
-    levels, rows, cols = alpha.shape[1:]
+    rows, cols = alpha.shape[2:]
     slots = GROUP * HB
-    g, steps = pl.program_id(0), pl.num_programs(0)
-    give = pltpu.make_async_copy(fine, fine_out, fine_sem)
-    slot = lax.rem(g, 2)
-
-    def store(step, l):
-        at = lax.rem(step, 2)
-        target = out.at[pl.ds(step * GROUP, GROUP), l]
-        return pltpu.make_async_copy(held.at[at, l], target, sem.at[at, l])
+    g = pl.program_id(0)
+    give = pltpu.make_async_copy(fine, fine_out, sem.at[0])
 
     @pl.when(g == 0)
     def _():
         give.start()
 
+    @pl.when(g == pl.num_programs(0) - 1)
+    def _():
+        give.wait()
+
     zero = jnp.zeros((cols, cols), BF16)
 
     def stack(high, low):
@@ -696,12 +694,7 @@
     lane = iota((rows, cols), 1)
     inner = (lane >= HB) & (lane < cols - HB)
     wide = iota((rows + 2 * HB, cols), 1)
-    for l in range(levels):
-
-        @pl.when(g >= 2)
-        def _(l=l):
-            store(g - 2, l).wait()
-
+    for l in range(alpha.shape[1]):
         res = residual[l]
         taps = lat[l, :, : 3 * (rows // 2 + 2 * HB)]
         side = jnp.where(wide // slots == l, west[g].astype(F32), east[g].astype(F32))
@@ -723,16 +716,7 @@
         for m in range(GROUP):
             turned = pltpu.roll(edge, (cols - HB - 2 * HB * m) % cols, 1)
             value = halves(total[m * rows : (m + 1) * rows]) + jnp.where(inner, 0.0, turned)
-            held[slot, l, m] = alpha[g * GROUP + m, l].astype(F32) + value
-        store(g, l).start()
-
-    @pl.when(g == steps - 1)
-    def _():
-        give.wait()
-        for l in range(levels):
-            store(g - 1, l).wait()
-        for l in range(levels):
-            store(g, l).wait()
+            out[m, l] = alpha[g * GROUP + m, l].astype(F32) + value
 
 
 def adjoint(alpha, perts, north, south, west, east, residual, lon, lat, fine):
@@ -741,16 +725,15 @@
         adjoint_kernel,
         grid=(members // GROUP,),
         in_specs=[pl.BlockSpec(memory_space=pltpu.VMEM)] * 10,
-        out_specs=[pl.BlockSpec(memory_space=pltpu.HBM)] * 2,
+        out_specs=[
+            pl.BlockSpec((GROUP, levels, rows, cols), lambda g: (g, 0, 0, 0)),
+            pl.BlockSpec(memory_space=pltpu.HBM),
+        ],
         out_shape=[
             jax.ShapeDtypeStruct(alpha.shape, F32),
             jax.ShapeDtypeStruct(fine.shape, F32),
         ],
-        scratch_shapes=[
-            pltpu.VMEM((2, levels, GROUP, rows, cols), F32),
-            pltpu.SemaphoreType.DMA((2, levels)),
-            pltpu.SemaphoreType.DMA,
-        ],
+        scratch_shapes=[pltpu.SemaphoreType.DMA((1,))],
         compiler_params=pltpu.CompilerParams(vmem_limit_bytes=BACK_LIMIT),
         cost_estimate=cost(members * levels * 2**25, alpha.size * 8),
     )(alpha, perts, north, south, west, east, residual, lon, lat, fine)

time: 35 us -> 32.8 us (0.937)
  Pallas kernels: 34.2 us -> 32 us
    pallas_call x1, Pallas kernels: 8.34 us -> 6.19 us  [adjoint(): pl.pallas_call(adjoint_kernel, grid=(members // GROUP,), in_specs=[pl.Blo...]
where the time goes in v5:
time: 32.8 us; the launch traced here: 32.7 us
  Pallas kernels  32 us (98%)
  between operations  0.64 us (2%)
    pallas_call x1, Pallas kernels, core_step(): pl.pallas_call(core_kernel, in_specs=[pl.BlockSpec(memory_space=pltpu.SME...  25.8 us
    pallas_call x1, Pallas kernels, adjoint(): pl.pallas_call(adjoint_kernel, grid=(members // GROUP,), in_specs=[pl.Blo...  6.19 us

profile of v5, /device:TPU:0, one launch (start us, length us, event | category | flops | bytes accessed | tf_op | source)
XLA Modules:
  0.0 32.7 jit_solution(2776705713295949101)
XLA Ops:
  0.6 25.8 %shard_map.104 = (f32[2,256,256]{2,1,0:T(8,128)S(1)}, f32[2,144,256]{2,1,0:T(8,128)S(1)}, bf16[40,2,128,128]{3,2,1,0:T(8,128)(2,1)S(1)}, bf16[40,2,128,128]{3,2,...) custom-call(s32[2]{0:T(128)} %widths.1, ...), custom_call_target="tpu_custom_call" | custom-call | flops 1073741824 | bytes 16777216 | tf_op jit(solution)/shard_map/pallas_call | solution.py:642
  26.5 6.2 %shard_map.105 = (f32[40,2,128,128]{3,2,1,0:T(8,128)}, f32[2,256,256]{2,1,0:T(8,128)}) custom-call(bf16[40,2,128,128]{3,2,1,0:T(8,128)(2,1)S(1)} %get-tuple-element.14.alpha, bf16[40,2,128,128]{3,2,1,0:T(8,128)(2,1)S(1)} %get-tuple-element.15.perts, bf16[40,2,8,128]{3,2,1,0:T(8,128)(2,1)S(1)} %get-tuple-element.16.north, ...), custom_call_target="tpu_custom_call" | custom-call | flops 2684354560 | bytes 10485760 | tf_op jit(solution)/shard_map/pallas_call | solution.py:724

commit v6 on v5

--- a/solution.py
+++ b/solution.py
@@ -251,15 +251,17 @@
 
     a_loads = [group_load(alpha, a_tile, g, 2 + steps) for g in range(steps)]
     p_arrive = []
-    def p_sides(g):
-        span = pl.ds(0, rows)
+    rim = STRIP - HB
+
+    def p_sides(groups, first, deep):
+        part, span = pl.ds(groups.start, groups.stop - groups.start), pl.ds(first, deep)
         pair = [
-            link("gx", 1, p_right.at[g], p_west.at[g, span]),
-            link("gx", -1, p_left.at[g], p_east.at[g, span]),
+            link("gx", 1, p_right.at[part, span], p_west.at[part, span]),
+            link("gx", -1, p_left.at[part, span], p_east.at[part, span]),
         ]
         for one in pair:
             one.start()
-        p_arrive.append(pair)
+        return pair
 
     for g in range(steps):
         p_loads[g].wait()
@@ -271,13 +273,16 @@
             met()
             for one in small + p_rows:
                 one.start()
-            p_sides(g)
+            rims = p_sides(range(1), 0, rows)
     corners = tilted(p_right, p_west, 1, 0, rows - HB, rows)
     corners += tilted(p_left, p_east, gxn - 1, 0, rows - HB, rows)
+    for first in (0, rows - rim):
+        rims += p_sides(range(1, steps), first, rim)
     for one in corners:
         one.start()
+    rims += corners
     for g in range(1, steps):
-        p_sides(g)
+        p_arrive.append(p_sides(range(g, g + 1), rim, rows - 2 * rim))
     for one in f_rows:
         one.start()
 
@@ -434,19 +439,7 @@
     for i in range(2):
         fine_wide[i, :, :fcols] = rows_of(fine_tile[i], f_low[i], f_high[i])
 
-    thick = iota((rows, cols), 1) // slots
-    thin = iota((2 * HB, cols), 1) // slots
-    side_sums = [None] * levels
-    for g in range(steps):
-        for one in p_arrive[g]:
-            one.arrive()
-        for l in range(levels):
-            west, east = p_west[g, :rows].astype(F32), p_east[g, :rows].astype(F32)
-            part = jnp.where(thick == l, west, east) * v_side[g, l, HB : HB + rows]
-            side_sums[l] = part if g == 0 else side_sums[l] + part
-    for one in corners:
-        one.arrive()
-    t_lane, e_lane = iota((t_rows, cols), 1), iota((e_rows, cols), 1)
+    t_lane = iota((t_rows, cols), 1)
 
     def fold(x, first, deep):
         total = None
@@ -460,25 +453,42 @@
         parts = [pltpu.roll(x, (first - b * REACH) % cols, 1) for b in range(start, start + blocks)]
         return rows_of(*parts)
 
+    def side_sum(total, l):
+        if l:
+            total = pltpu.roll(total, slots, 1)
+        for shift in (HB, 2 * HB, 4 * HB):
+            total = total + pltpu.roll(total, shift, 1)
+        return total
+
+    def products(l, g, take, v):
+        west, east = take(p_west.at[g]).astype(F32), take(p_east.at[g]).astype(F32)
+        return jnp.where(iota(west.shape, 1) // slots == l, west, east) * v
+
+    def outward(core, side):
+        lane_at = iota(side.shape, 1)
+        eastward = jnp.where(lane_at >= cols - HB, side, pltpu.roll(core, cols - HB, 1))
+        westward = jnp.where(lane_at < slots, side, pltpu.roll(core, slots, 1))
+        return (eastward, cols - REACH), (westward, slots - HB)
+
+    def rim_of(part):
+        far = part[rows:].astype(F32)
+        near = [part[:rim].astype(F32), part[rows - rim : rows].astype(F32)]
+        return rows_of(far[:HB], *near, far[HB:])
+
+    for one in rims:
+        one.arrive()
     for l in range(levels):
-        ends = None
+        total = None
         for g in range(steps):
-            west, east = p_west[g, rows:].astype(F32), p_east[g, rows:].astype(F32)
-            v = rows_of(v_side[g, l, :HB], v_side[g, l, HB + rows :])
-            part = jnp.where(thin == l, west, east) * v
-            ends = part if ends is None else ends + part
-        side = rows_of(ends[:HB], side_sums[l], ends[HB:])
-        if l:
-            side = pltpu.roll(side, slots, 1)
-        for shift in (HB, 2 * HB, 4 * HB):
-            side = side + pltpu.roll(side, shift, 1)
-        ext[l, :, cols:] = side
-        core = ext[l, :, :cols]
-        eastward = jnp.where(e_lane >= cols - HB, side, pltpu.roll(core, cols - HB, 1))
-        westward = jnp.where(e_lane < slots, side, pltpu.roll(core, slots, 1))
-        for i, (x, first) in enumerate(((eastward, cols - REACH), (westward, slots - HB))):
-            flank[l, i] = fold(x, first, STRIP)
-            tip[l, i] = fold(rows_of(x[e_rows - STRIP :], x[:STRIP]), first, HB)
+            v = rows_of(v_side[g, l, :STRIP], v_side[g, l, e_rows - STRIP :])
+            part = products(l, g, rim_of, v)
+            total = part if total is None else total + part
+        total = side_sum(total, l)
+        ext[l, :STRIP, cols:] = total[:STRIP]
+        ext[l, e_rows - STRIP :, cols:] = total[STRIP:]
+        core = rows_of(ext[l, :STRIP, :cols], ext[l, e_rows - STRIP :, :cols])
+        for i, (x, first) in enumerate(outward(core, total)):
+            tip[l, i] = fold(rows_of(x[STRIP:], x[:STRIP]), first, HB)
 
     corner_links, side_links, end_links, swaps = [], [], [], []
     for s in range(count):
@@ -493,9 +503,28 @@
                 corner_links.append(link("gy", turn, tip.at[peer, i], tips.at[s, i, j], at))
         if s:
             swaps.append(link("ma", peer - ma, ext.at[peer], other.at[s - 1]))
-    sent = corner_links + side_links + end_links + swaps
-    for one in sent + f_arrive:
+    for one in corner_links + end_links:
         one.start()
+    inside = slice(STRIP, e_rows - STRIP)
+    side_sums = [None] * levels
+    for g in range(steps):
+        if g:
+            for one in p_arrive[g - 1]:
+                one.arrive()
+        for l in range(levels):
+            part = products(l, g, lambda x: x[rim : rows - rim], v_side[g, l, inside])
+            side_sums[l] = part if g == 0 else side_sums[l] + part
+    for l in range(levels):
+        ext[l, inside, cols:] = side_sum(side_sums[l], l)
+        for i, (x, first) in enumerate(outward(ext[l, :, :cols], ext[l, :, cols:])):
+            flank[l, i] = fold(x, first, STRIP)
+    sent = corner_links + end_links + side_links + swaps
+    late = side_links + swaps + f_arrive
+    for one in late:
+        one.start()
+    for one in pending:
+        if one not in late:
+            one.sent()
     for one in sent:
         one.arrive()
     mine, strips_in, flank_in, tip_in = ext[ma], ends_in[0], flanks[0], tips[0]
@@ -561,9 +590,11 @@
     across = dot3((down_lat[0], down_lat[1]), split(misfit))
     residual[ma] = dot3(split(across), (down_lon[0], down_lon[1]))
     share(residual)
+    for one in late:
+        one.sent()
     for one in final:
         one.arrive()
-    for one in pending:
+    for one in final:
         one.sent()
 
 

time: 32.8 us -> 32 us (0.976)
  Pallas kernels: 32 us -> 31.2 us
    pallas_call x1, Pallas kernels: 25.8 us -> 25 us  [core_step(): pl.pallas_call(core_kernel, in_specs=[pl.BlockSpec(memory_space=pltpu.SME...]
where the time goes in v6:
time: 32 us; the launch traced here: 31.8 us
  Pallas kernels  31.2 us (98%)
  between operations  0.64 us (2%)
    pallas_call x1, Pallas kernels, core_step(): pl.pallas_call(core_kernel, in_specs=[pl.BlockSpec(memory_space=pltpu.SME...  25 us
    pallas_call x1, Pallas kernels, adjoint(): pl.pallas_call(adjoint_kernel, grid=(members // GROUP,), in_specs=[pl.Blo...  6.2 us

profile of v6, /device:TPU:0, one launch (start us, length us, event | category | flops | bytes accessed | tf_op | source)
XLA Modules:
  0.0 31.8 jit_solution(11328092692378595384)
XLA Ops:
  0.6 25.0 %shard_map.104 = (f32[2,256,256]{2,1,0:T(8,128)S(1)}, f32[2,144,256]{2,1,0:T(8,128)S(1)}, bf16[40,2,128,128]{3,2,1,0:T(8,128)(2,1)S(1)}, bf16[40,2,128,128]{3,2,...) custom-call(s32[2]{0:T(128)} %widths.1, ...), custom_call_target="tpu_custom_call" | custom-call | flops 1073741824 | bytes 16777216 | tf_op jit(solution)/shard_map/pallas_call | solution.py:673
  25.6 6.2 %shard_map.105 = (f32[40,2,128,128]{3,2,1,0:T(8,128)}, f32[2,256,256]{2,1,0:T(8,128)}) custom-call(bf16[40,2,128,128]{3,2,1,0:T(8,128)(2,1)S(1)} %get-tuple-element.14.alpha, bf16[40,2,128,128]{3,2,1,0:T(8,128)(2,1)S(1)} %get-tuple-element.15.perts, bf16[40,2,8,128]{3,2,1,0:T(8,128)(2,1)S(1)} %get-tuple-element.16.north, ...), custom_call_target="tpu_custom_call" | custom-call | flops 2684354560 | bytes 10485760 | tf_op jit(solution)/shard_map/pallas_call | solution.py:755

commit v7 on v6

--- a/solution.py
+++ b/solution.py
@@ -159,9 +159,9 @@
 
 
 def core_kernel(
-    widths, lat_i, lat_w, lon_i, lon_w, alpha, perts, innov, weight,
+    widths_in, lat_i_in, lat_w_in, lon_i_in, lon_w_in, alpha, perts, innov, weight,
     increment, residual, a_tile, p_tile, p_north, p_south, p_west, p_east, lon_taps, lat_back,
-    fine_tile, pick, edge_taps, lat_fore, v_strip, v_side, p_right, p_left,
+    widths, lat_i, lat_w, lon_i, lon_w, fine_tile, pick, edge_taps, lat_fore, v_strip, v_side, p_right, p_left,
     f_low, f_high, f_right, f_left, f_west, f_east, fine_wide,
     lat_i_low, lat_i_high, lat_w_low, lat_w_high, lon_i_west, lon_i_east, lon_w_west, lon_w_east,
     up_lon, up_lat, down_lat, down_lon, ext, other, ends_in, flank, tip, flanks, tips,
@@ -173,6 +173,13 @@
     ma, count = lax.axis_index("ma"), lax.axis_size("ma")
     gx, gxn = lax.axis_index("gx"), lax.axis_size("gx")
     met = greet()
+    tables = ((widths_in, widths), (lat_i_in, lat_i), (lat_w_in, lat_w), (lon_i_in, lon_i), (lon_w_in, lon_w))
+    t_loads = [
+        pltpu.make_async_copy(src, dst, local.at[2 + 2 * steps + i])
+        for i, (src, dst) in enumerate(tables)
+    ]
+    for load in t_loads:
+        load.start()
     f_loads = [
         pltpu.make_async_copy(src.at[ma], fine_tile.at[i], local.at[i])
         for i, src in enumerate((innov, weight))
@@ -270,6 +277,8 @@
         p_right[g] = both[:, :cols]
         p_left[g] = both[:, cols:]
         if g == 0:
+            for load in t_loads:
+                load.wait()
             met()
             for one in small + p_rows:
                 one.start()
@@ -633,6 +642,10 @@
     fine_side = ((-(-frows // (FOLD * HB)) * HB + 2 * HB, cols), F32)
     packed = ((steps, rows, cols), BF16)
     scratch = [
+        (lat_i.shape, jnp.int32),
+        (lat_w.shape, F32),
+        (lon_i.shape, jnp.int32),
+        (lon_w.shape, F32),
         ((2, frows, fcols), F32),
         ((levels * GROUP // 2, 2 * cols, 2 * cols), BF16),
         ((levels, 2, cols, cols), BF16),
@@ -672,14 +685,15 @@
     anywhere = pl.BlockSpec(memory_space=pltpu.HBM)
     return pl.pallas_call(
         core_kernel,
-        in_specs=[pl.BlockSpec(memory_space=pltpu.SMEM)] + [vmem] * 4 + [anywhere] * 4,
+        in_specs=[anywhere] * 9,
         out_specs=[vmem] * len(outs),
         out_shape=[pltpu.VMEM(shape, kind) for shape, kind in outs],
-        scratch_shapes=[pltpu.VMEM(shape, kind) for shape, kind in scratch]
+        scratch_shapes=[pltpu.SMEM(widths.shape, jnp.int32)]
+        + [pltpu.VMEM(shape, kind) for shape, kind in scratch]
         + [
             pltpu.SemaphoreType.DMA((96,)),
             pltpu.SemaphoreType.DMA((96,)),
-            pltpu.SemaphoreType.DMA((2 + 2 * steps,)),
+            pltpu.SemaphoreType.DMA((7 + 2 * steps,)),
         ],
         compiler_params=pltpu.CompilerParams(
             collective_id=0, has_side_effects=True, vmem_limit_bytes=VMEM_BYTES - VMEM_SLACK - kept

time: 32 us -> 31.2 us (0.975)
  Pallas kernels: 31.2 us -> 30.4 us
    pallas_call x1, Pallas kernels: 25 us -> 24.2 us  [core_step(): pl.pallas_call(core_kernel, in_specs=[anywhere] * 9, out_specs=[vmem] * l...]
where the time goes in v7:
time: 31.2 us; the launch traced here: 31.1 us
  Pallas kernels  30.4 us (97%)
  between operations  0.64 us (2%)
    pallas_call x1, Pallas kernels, core_step(): pl.pallas_call(core_kernel, in_specs=[anywhere] * 9, out_specs=[vmem] * l...  24.2 us
    pallas_call x1, Pallas kernels, adjoint(): pl.pallas_call(adjoint_kernel, grid=(members // GROUP,), in_specs=[pl.Blo...  6.2 us

profile of v7, /device:TPU:0, one launch (start us, length us, event | category | flops | bytes accessed | tf_op | source)
XLA Modules:
  0.0 31.1 jit_solution(17512161238537204542)
XLA Ops:
  0.6 24.2 %shard_map.104 = (f32[2,256,256]{2,1,0:T(8,128)S(1)}, f32[2,144,256]{2,1,0:T(8,128)S(1)}, bf16[40,2,128,128]{3,2,1,0:T(8,128)(2,1)S(1)}, bf16[40,2,128,128]{3,2,...) custom-call(s32[2]{0:T(128)} %widths_in.1, ...), custom_call_target="tpu_custom_call" | custom-call | flops 1073741824 | bytes 16777216 | tf_op jit(solution)/shard_map/pallas_call | solution.py:686
  24.9 6.2 %shard_map.105 = (f32[40,2,128,128]{3,2,1,0:T(8,128)}, f32[2,256,256]{2,1,0:T(8,128)}) custom-call(bf16[40,2,128,128]{3,2,1,0:T(8,128)(2,1)S(1)} %get-tuple-element.14.alpha, bf16[40,2,128,128]{3,2,1,0:T(8,128)(2,1)S(1)} %get-tuple-element.15.perts, bf16[40,2,8,128]{3,2,1,0:T(8,128)(2,1)S(1)} %get-tuple-element.16.north, ...), custom_call_target="tpu_custom_call" | custom-call | flops 2684354560 | bytes 10485760 | tf_op jit(solution)/shard_map/pallas_call | solution.py:769

commit v8 on v7

--- a/solution.py
+++ b/solution.py
@@ -140,19 +140,21 @@
     def hail(device):
         pl.semaphore_signal(barrier, inc=1, device_id=device, device_id_type=MESH)
 
-    for s in range(count):
-        peer = lax.rem(ma + s, count)
-        if s:
-            hail({"ma": peer})
-        sides = [lax.rem(gx + step, gxn) for step in (1, gxn - 1)]
-        for side in sides:
+    peers = [lax.rem(ma + s, count) for s in range(count)]
+    sides = [lax.rem(gx + step, gxn) for step in (1, gxn - 1)]
+    for step, there in ((-1, gy > 0), (1, gy < gyn - 1)):
+
+        @pl.when(there)
+        def _(step=step):
+            for side in (*sides, gx):
+                for peer in peers[::-1]:
+                    hail({"gx": side, "gy": gy + step, "ma": peer})
+
+    for side in sides:
+        for peer in peers[::-1]:
             hail({"gx": side, "ma": peer})
-        for step, there in ((-1, gy > 0), (1, gy < gyn - 1)):
-
-            @pl.when(there)
-            def _(step=step, peer=peer, sides=sides):
-                for side in (gx, *sides):
-                    hail({"gx": side, "gy": gy + step, "ma": peer})
+    for peer in peers[1:]:
+        hail({"ma": peer})
 
     below, above = jnp.minimum(gy, 1), jnp.minimum(gyn - 1 - gy, 1)
     return lambda: pl.semaphore_wait(barrier, 3 * count - 1 + (below + above) * 3 * count)

time: 31.2 us -> 31.1 us (level)
  no operation moved by 1% of the time
where the time goes in v8:
time: 31.1 us; the launch traced here: 30.9 us
  Pallas kernels  30.3 us (97%)
  between operations  0.64 us (2%)
    pallas_call x1, Pallas kernels, core_step(): pl.pallas_call(core_kernel, in_specs=[anywhere] * 9, out_specs=[vmem] * l...  24.1 us
    pallas_call x1, Pallas kernels, adjoint(): pl.pallas_call(adjoint_kernel, grid=(members // GROUP,), in_specs=[pl.Blo...  6.19 us

profile of v8, /device:TPU:0, one launch (start us, length us, event | category | flops | bytes accessed | tf_op | source)
XLA Modules:
  0.0 30.9 jit_solution(7386651848776021083)
XLA Ops:
  0.6 24.1 %shard_map.104 = (f32[2,256,256]{2,1,0:T(8,128)S(1)}, f32[2,144,256]{2,1,0:T(8,128)S(1)}, bf16[40,2,128,128]{3,2,1,0:T(8,128)(2,1)S(1)}, bf16[40,2,128,128]{3,2,...) custom-call(s32[2]{0:T(128)} %widths_in.1, ...), custom_call_target="tpu_custom_call" | custom-call | flops 1073741824 | bytes 16777216 | tf_op jit(solution)/shard_map/pallas_call | solution.py:688
  24.7 6.2 %shard_map.105 = (f32[40,2,128,128]{3,2,1,0:T(8,128)}, f32[2,256,256]{2,1,0:T(8,128)}) custom-call(bf16[40,2,128,128]{3,2,1,0:T(8,128)(2,1)S(1)} %get-tuple-element.14.alpha, bf16[40,2,128,128]{3,2,1,0:T(8,128)(2,1)S(1)} %get-tuple-element.15.perts, bf16[40,2,8,128]{3,2,1,0:T(8,128)(2,1)S(1)} %get-tuple-element.16.north, ...), custom_call_target="tpu_custom_call" | custom-call | flops 2684354560 | bytes 10485760 | tf_op jit(solution)/shard_map/pallas_call | solution.py:771
